TPU v7x, 512 devices: a whole 4x8x8 slice. The times are simulated.
512 devices in a mesh: gz: 256 (over x, z, y), col: 2 (over core).
Axes of the slice: x: 4, y: 8, z: 8, core: 2. Of those that a mesh axis runs over, the one named last changes fastest.
Arguments:
- velocity: float32 [1024, 3, 128, 128], P('gz', None, 'col'), may hold values from -6 to 6
- forces: float32 [3, 2097152], P(None, ('gz', 'col')), may hold values from -60 to 60
- offsets: float32 [3, 2097152], P(None, ('gz', 'col')), may hold values from 0 to 1
- cell_x: int32 [2097152], P(('gz', 'col')), may hold values from 0 to 127
- cell_y: int32 [2097152], P(('gz', 'col')), may hold values from 0 to 127
- cell_z: int32 [2097152], P(('gz', 'col')), may hold values from 0 to 12
- band_start: int32 [256], P('gz'), may hold values from 0 to 255, as said below
Outputs:
- force_field: float32 [1024, 3, 128, 128], P('gz', None, 'col')
- velocity_next: float32 [1024, 3, 128, 128], P('gz', None, 'col')
Inputs may be any that keep to these rules, and one draw needn't show every extreme that they name: (g - band_start[g]) mod 256 lies in 0 to 3 for every gz index g.
All inputs are finite; a program needn't handle non-finite values.
Results may differ from a plain program's by a relative error of at most 0.0037.
Values sent between devices are 32-bit elements; how exact they have to be, the bound alone decides.
No kernel may reach another device: no remote copies, remote signals or barrier semaphores. Data moves between devices by JAX's collectives and lax.ppermute only.
A program may use at most 64 MiB of HBM per device.

v0:
```python
import math

import jax
import jax.numpy as jnp
from jax import lax
from jax.sharding import PartitionSpec as P

BAND = 4


viscous = 0.15


def side_by_side(arrays, axis, dim, along):
    both = jnp.concatenate(arrays, axis=along)
    filled, at, outs = (lax.all_gather(both, axis, axis=dim, tiled=True), 0, [])
    for a in arrays:
        outs.append(lax.slice_in_dim(filled, at, at + a.shape[along], axis=along))
        at += a.shape[along]
    return tuple(outs)


def shifted(x, axis, by):
    devices = lax.axis_size(axis)
    return lax.ppermute(x, axis, [(i, (i + by) % devices) for i in range(devices)])


def with_halo(x, sides, width):
    edges = {}
    for axis, dim in sides:
        devices, length = (lax.axis_size(axis), x.shape[dim])
        up = [(i, (i + 1) % devices) for i in range(devices)]
        last = lax.slice_in_dim(x, length - width, length, axis=dim)
        leading = lax.slice_in_dim(x, 0, width, axis=dim)
        edges[dim] = (
            lax.ppermute(last, axis, up),
            lax.ppermute(leading, axis, [(b, a) for a, b in up]),
        )
    done = []
    for _, dim in sides:
        low, high = edges[dim]
        around = [(width, width) if d in done else (0, 0) for d in range(x.ndim)]
        x = jnp.concatenate([jnp.pad(low, around), x, jnp.pad(high, around)], axis=dim)
        done.append(dim)
    return x


def delta_weights(fraction):
    root_term = jnp.sqrt(1.0 + 4.0 * fraction - 4.0 * fraction * fraction)
    return jnp.stack(
        [
            (3.0 - 2.0 * fraction - root_term) / 8.0,
            (3.0 - 2.0 * fraction + root_term) / 8.0,
            (1.0 + 2.0 * fraction + root_term) / 8.0,
            (1.0 + 2.0 * fraction - root_term) / 8.0,
        ]
    )


def hit_matrix(points, weights, columns, period):
    result = jnp.zeros((points.shape[0], columns.shape[0]), jnp.float32)
    for corner in range(4):
        target = (points + corner) % period
        result = result + jnp.where(
            columns[None, :] == target[:, None], weights[corner][:, None], 0.0
        )
    return result


def spread_band(
    forces, offsets, cell_x, cell_y, cell_z, first_x, span_x, full_x, width_y, band_depth
):
    marker_count = cell_x.shape[0]
    block_size = math.gcd(marker_count, 256)
    turn_count = marker_count // block_size
    x_columns = first_x + jnp.arange(span_x, dtype=jnp.int32)
    y_columns = jnp.arange(width_y, dtype=jnp.int32)
    z_columns = jnp.arange(band_depth, dtype=jnp.int32)

    def one_block(totals, pieces):
        piece_x, piece_y, piece_z, piece_offsets, piece_forces = pieces
        x_weights = hit_matrix(piece_x, delta_weights(piece_offsets[0]), x_columns, full_x)
        y_weights = hit_matrix(piece_y, delta_weights(piece_offsets[1]), y_columns, width_y).astype(
            jnp.bfloat16
        )
        z_weights = hit_matrix(piece_z, delta_weights(piece_offsets[2]), z_columns, band_depth)
        scaled = (
            z_weights[:, :, None, None]
            * piece_forces.T[:, None, :, None]
            * x_weights[:, None, None, :]
        )
        scaled = scaled.reshape(block_size, band_depth * 3 * span_x).astype(jnp.bfloat16)
        product = lax.dot_general(
            scaled, y_weights, (((0,), (0,)), ((), ())), preferred_element_type=jnp.float32
        )
        return (totals + product, None)

    pieces = (
        cell_x.reshape(turn_count, block_size),
        cell_y.reshape(turn_count, block_size),
        cell_z.reshape(turn_count, block_size),
        offsets.reshape(3, turn_count, block_size).transpose(1, 0, 2),
        forces.reshape(3, turn_count, block_size).transpose(1, 0, 2),
    )
    totals = jnp.zeros((band_depth * 3 * span_x, width_y), jnp.float32)
    totals = lax.scan(one_block, totals, pieces)[0]
    return totals.reshape(band_depth, 3, span_x, width_y)


def on_device(velocity, forces, offsets, cell_x, cell_y, cell_z, band_start):
    slab_depth, components, half_x, width_y = velocity.shape
    gz_count = lax.axis_size("gz")
    gz_index = lax.axis_index("gz")
    col_index = lax.axis_index("col")
    full_x = half_x * lax.axis_size("col")
    band_depth = BAND * slab_depth
    cell_x, cell_y, cell_z, offsets, forces = (
        lax.all_gather(cell_x, "col", axis=0, tiled=True),
        lax.all_gather(cell_y, "col", axis=0, tiled=True),
        lax.all_gather(cell_z, "col", axis=0, tiled=True),
        *side_by_side((offsets, forces), "col", 1, 0),
    )
    band_field = spread_band(
        forces,
        offsets,
        cell_x,
        cell_y,
        cell_z,
        col_index * half_x,
        half_x,
        full_x,
        width_y,
        band_depth,
    )
    behind = (gz_index - band_start[0]) % gz_count
    window = jnp.zeros(((2 * BAND - 1) * slab_depth, components, half_x, width_y), jnp.float32)
    window = lax.dynamic_update_slice_in_dim(
        window, band_field, (BAND - 1 - behind) * slab_depth, 0
    )
    center = window[(BAND - 1) * slab_depth : BAND * slab_depth]
    own_slabs = center
    for offset in range(1, BAND):
        from_below = shifted(
            window[(BAND - 1 + offset) * slab_depth : (BAND + offset) * slab_depth], "gz", offset
        )
        from_above = shifted(
            window[(BAND - 1 - offset) * slab_depth : (BAND - offset) * slab_depth], "gz", -offset
        )
        own_slabs = own_slabs + from_below + from_above
    padded = with_halo(velocity, (("gz", 0), ("col", 2)), 1)
    neighbours = padded[2:, :, 1:-1] + padded[:-2, :, 1:-1]
    neighbours = neighbours + padded[1:-1, :, 2:] + padded[1:-1, :, :-2]
    neighbours = neighbours + jnp.roll(velocity, 1, 3) + jnp.roll(velocity, -1, 3)
    velocity_next = velocity + viscous * (neighbours - 6.0 * velocity) + own_slabs
    return (own_slabs, velocity_next)


def solution(mesh):
    in_specs = (
        P("gz", None, "col", None),
        P(None, ("gz", "col")),
        P(None, ("gz", "col")),
        P(("gz", "col")),
        P(("gz", "col")),
        P(("gz", "col")),
        P("gz"),
    )
    out_specs = (P("gz", None, "col", None), P("gz", None, "col", None))
    return jax.shard_map(
        on_device, mesh=mesh, in_specs=in_specs, out_specs=out_specs, check_vma=False
    )
```

profile of v0, /device:TPU:1, one launch (start us, length us, event | category | flops | bytes accessed | tf_op | source)
XLA Modules:
  0.0 152.0 jit_solution(5021726263059532782)
XLA Ops:
  1.3 0.9 pad_maximum_fusion.4
  2.2 8.5 %all_gather.13 = f32[6,8192]{1,0:T(8,128)S(1)} all-gather(f32[6,4096]{1,0:T(8,128)S(1)} %pad_maximum_fusion.4), channel_id=1, replica_groups=mesh['gz'=256,'col'=2] {'col'}, dimensions={1}, use_global_device_ids=true | all-gather | bytes 294912 | tf_op jit(solution)/shard_map/all_gather | solution.py:16
  10.7 2.1 %all_gather.12 = s32[8192]{0:T(1024)S(1)} all-gather(s32[4096]{0:T(1024)} %param.14), channel_id=1, replica_groups=mesh['gz'=256,'col'=2] {'col'}, dimensions={0}, use_global_device_ids=true | all-gather | bytes 49152 | tf_op jit(solution)/shard_map/all_gather | solution.py:120
  12.8 2.0 %all_gather.14 = s32[8192]{0:T(1024)S(1)} all-gather(s32[4096]{0:T(1024)} %param.12), channel_id=1, replica_groups=mesh['gz'=256,'col'=2] {'col'}, dimensions={0}, use_global_device_ids=true | all-gather | bytes 49152 | tf_op jit(solution)/shard_map/all_gather | solution.py:118
  14.9 2.0 %all_gather.15 = s32[8192]{0:T(1024)S(1)} all-gather(s32[4096]{0:T(1024)} %param.13), channel_id=1, replica_groups=mesh['gz'=256,'col'=2] {'col'}, dimensions={0}, use_global_device_ids=true | all-gather | bytes 49152 | tf_op jit(solution)/shard_map/all_gather | solution.py:119
  16.9 61.3 %while.15 = (s32[]{:T(128)}, f32[3072,128]{1,0:T(8,128)S(1)}, s32[32,256]{1,0:T(8,128)S(1)}, f32[32,3,256]{2,1,0:T(4,128)S(1)}, f32[32,3,256]{2,1,0:T(4,128)S(1)...) while((s32[]{:T(128)}, f32[3072,128]{1,0:T(8,128)S(1)}, ...), condition=%wide.region_1.2_spmd.clone.clone, body=%wide.region_0.1_spmd.clone.clone.sunk | while | flops 204364352 | bytes 6631091 | solution.py:106
  17.8 1.0 convolution_add_fusion.2
  19.2 0.5 multiply_convert_fusion.2
  19.7 1.0 convolution_add_fusion.2
  21.6 1.0 convolution_add_fusion.2
  23.6 1.0 convolution_add_fusion.2
  25.5 1.0 convolution_add_fusion.2
  27.4 1.0 convolution_add_fusion.2
  29.3 1.0 convolution_add_fusion.2
  30.7 0.5 multiply_convert_fusion.2
  31.2 1.0 convolution_add_fusion.2
  33.1 1.0 convolution_add_fusion.2
  34.5 0.5 multiply_convert_fusion.2
  35.1 1.0 convolution_add_fusion.2
  37.0 1.0 convolution_add_fusion.2
  38.3 0.5 multiply_convert_fusion.2
  38.9 1.0 convolution_add_fusion.2
  40.8 1.0 convolution_add_fusion.2
  42.2 0.5 multiply_convert_fusion.2
  42.7 1.0 convolution_add_fusion.2
  44.6 1.0 convolution_add_fusion.2
  46.0 0.5 multiply_convert_fusion.2
  46.5 1.0 convolution_add_fusion.2
  47.9 0.5 multiply_convert_fusion.2
  48.5 1.0 convolution_add_fusion.2
  49.8 0.5 multiply_convert_fusion.2
  50.4 1.0 convolution_add_fusion.2
  51.7 0.5 multiply_convert_fusion.2
  52.3 1.0 convolution_add_fusion.2
  53.7 0.5 multiply_convert_fusion.2
  54.2 1.0 convolution_add_fusion.2
  55.6 0.5 multiply_convert_fusion.2
  56.1 1.0 convolution_add_fusion.2
  58.0 1.0 convolution_add_fusion.2
  59.4 0.5 multiply_convert_fusion.2
  60.0 1.0 convolution_add_fusion.2
  61.9 1.0 convolution_add_fusion.2
  63.8 1.0 convolution_add_fusion.2
  65.7 1.0 convolution_add_fusion.2
  67.6 1.0 convolution_add_fusion.2
  69.5 1.0 convolution_add_fusion.2
  71.5 1.0 convolution_add_fusion.2
  73.4 1.0 convolution_add_fusion.2
  75.3 1.0 convolution_add_fusion.2
  77.2 1.0 convolution_add_fusion.2
  78.9 1.9 %collective-permute-start = (f32[4,3,64,128]{3,2,1,0:T(8,128)S(1)}, f32[4,3,64,128]{3,2,1,0:T(8,128)S(1)}, u32[]{:S(2)}, u32[]{:S(2)}) collective-permute-start(f32[4,3,64,128]{3,2,1,0:T(8,128)S(1)} %get-tuple-element.290), channel_id=1, source_target_pairs={{0,2},{2,4},{4,6},{6,8},{8,10},{10,12},{12,14},{14,16},{16,18},{18... | collective-permute-start | bytes 1179656 | tf_op jit(solution)/shard_map/ppermute | solution.py:25
  80.9 1.9 %collective-permute-start.7 = (f32[1,3,64,128]{3,2,1,0:T(8,128)S(1)}, f32[1,3,64,128]{3,2,1,0:T(8,128)S(1)}, u32[]{:S(2)}, u32[]{:S(2)}) collective-permute-start(f32[1,3,64,128]{3,2,1,0:T(8,128)S(1)} %get-tuple-element.303), channel_id=1, source_target_pairs={{0,2},{2,4},{4,6},{6,8},{8,10},{10,12},{12,14},{14,16},{16,18},{18... | collective-permute-start | bytes 294920 | tf_op jit(solution)/shard_map/ppermute | solution.py:36
  82.8 10.4 %collective-permute-start.6 = (f32[1,3,64,128]{3,2,1,0:T(8,128)S(1)}, f32[1,3,64,128]{3,2,1,0:T(8,128)S(1)}, u32[]{:S(2)}, u32[]{:S(2)}) collective-permute-start(f32[1,3,64,128]{3,2,1,0:T(8,128)S(1)} %get-tuple-element.302), channel_id=1, source_target_pairs={{2,0},{4,2},{6,4},{8,6},{10,8},{12,10},{14,12},{16,14},{18,16},{20... | collective-permute-start | bytes 294920 | tf_op jit(solution)/shard_map/ppermute | solution.py:37
  93.2 2.5 %collective-permute-start.8 = (f32[4,3,1,128]{3,2,1,0:T(1,128)S(1)}, f32[4,3,1,128]{3,2,1,0:T(1,128)S(1)}, u32[]{:S(2)}, u32[]{:S(2)}) collective-permute-start(f32[4,3,1,128]{3,2,1,0:T(1,128)S(1)} %get-tuple-element.300), channel_id=1, source_target_pairs={{1,0},{0,1},{3,2},{2,3},{5,4},{4,5},{7,6},{6,7},{9,8},{8,9},{11,10... | collective-permute-start | bytes 18440 | tf_op jit(solution)/shard_map/ppermute | solution.py:37
  95.8 1.9 %collective-permute-start.9 = (f32[4,3,1,128]{3,2,1,0:T(1,128)S(1)}, f32[4,3,1,128]{3,2,1,0:T(1,128)S(1)}, u32[]{:S(2)}, u32[]{:S(2)}) collective-permute-start(f32[4,3,1,128]{3,2,1,0:T(1,128)S(1)} %get-tuple-element.301), channel_id=1, source_target_pairs={{0,1},{1,0},{2,3},{3,2},{4,5},{5,4},{6,7},{7,6},{8,9},{9,8},{10,11... | collective-permute-start | bytes 18440 | tf_op jit(solution)/shard_map/ppermute | solution.py:36
  97.9 3.6 %collective-permute-start.1 = (f32[4,3,64,128]{3,2,1,0:T(8,128)S(1)}, f32[4,3,64,128]{3,2,1,0:T(8,128)S(1)}, u32[]{:S(2)}, u32[]{:S(2)}) collective-permute-start(f32[4,3,64,128]{3,2,1,0:T(8,128)S(1)} %get-tuple-element.295), channel_id=1, source_target_pairs={{0,510},{2,0},{4,2},{6,4},{8,6},{10,8},{12,10},{14,12},{16,14},{18... | collective-permute-start | bytes 1179656 | tf_op jit(solution)/shard_map/ppermute | solution.py:25
  101.6 1.9 %collective-permute-start.2 = (f32[4,3,64,128]{3,2,1,0:T(8,128)S(1)}, f32[4,3,64,128]{3,2,1,0:T(8,128)S(1)}, u32[]{:S(2)}, u32[]{:S(2)}) collective-permute-start(f32[4,3,64,128]{3,2,1,0:T(8,128)S(1)} %get-tuple-element.294), channel_id=1, source_target_pairs={{0,4},{2,6},{4,8},{6,10},{8,12},{10,14},{12,16},{14,18},{16,20},{1... | collective-permute-start | bytes 1179656 | tf_op jit(solution)/shard_map/ppermute | solution.py:25
  103.5 9.7 %collective-permute-start.3 = (f32[4,3,64,128]{3,2,1,0:T(8,128)S(1)}, f32[4,3,64,128]{3,2,1,0:T(8,128)S(1)}, u32[]{:S(2)}, u32[]{:S(2)}) collective-permute-start(f32[4,3,64,128]{3,2,1,0:T(8,128)S(1)} %get-tuple-element.293), channel_id=1, source_target_pairs={{0,508},{2,510},{4,0},{6,2},{8,4},{10,6},{12,8},{14,10},{16,12},{1... | collective-permute-start | bytes 1179656 | tf_op jit(solution)/shard_map/ppermute | solution.py:25
  113.2 1.9 %collective-permute-start.4 = (f32[4,3,64,128]{3,2,1,0:T(8,128)S(1)}, f32[4,3,64,128]{3,2,1,0:T(8,128)S(1)}, u32[]{:S(2)}, u32[]{:S(2)}) collective-permute-start(f32[4,3,64,128]{3,2,1,0:T(8,128)S(1)} %get-tuple-element.292), channel_id=1, source_target_pairs={{0,6},{2,8},{4,10},{6,12},{8,14},{10,16},{12,18},{14,20},{16,22},{... | collective-permute-start | bytes 1179656 | tf_op jit(solution)/shard_map/ppermute | solution.py:25
  115.2 10.6 %collective-permute-start.5 = (f32[4,3,64,128]{3,2,1,0:T(8,128)S(1)}, f32[4,3,64,128]{3,2,1,0:T(8,128)S(1)}, u32[]{:S(2)}, u32[]{:S(2)}) collective-permute-start(f32[4,3,64,128]{3,2,1,0:T(8,128)S(1)} %get-tuple-element.291), channel_id=1, source_target_pairs={{0,506},{2,508},{4,510},{6,0},{8,2},{10,4},{12,6},{14,8},{16,10},{... | collective-permute-start | bytes 1179656 | tf_op jit(solution)/shard_map/ppermute | solution.py:25
  126.0 4.3 %collective-permute-done.2 = f32[4,3,64,128]{3,2,1,0:T(8,128)S(1)} collective-permute-done((f32[4,3,64,128]{3,2,1,0:T(8,128)S(1)}, f32[4,3,64,128]{3,2,1,0:T(8,128)S(1)}, u32[]{:S(2)}, u32[]{:S(2)}) %collective-permute-start.2) | collective-permute-done | bytes 393248 | tf_op jit(solution)/shard_map/ppermute | solution.py:25
  130.3 10.0 %collective-permute-done.3 = f32[4,3,64,128]{3,2,1,0:T(8,128)S(1)} collective-permute-done((f32[4,3,64,128]{3,2,1,0:T(8,128)S(1)}, f32[4,3,64,128]{3,2,1,0:T(8,128)S(1)}, u32[]{:S(2)}, u32[]{:S(2)}) %collective-permute-start.3) | collective-permute-done | bytes 393248 | tf_op jit(solution)/shard_map/ppermute | solution.py:25
  140.3 10.2 %collective-permute-done.4 = f32[4,3,64,128]{3,2,1,0:T(8,128)S(1)} collective-permute-done((f32[4,3,64,128]{3,2,1,0:T(8,128)S(1)}, f32[4,3,64,128]{3,2,1,0:T(8,128)S(1)}, u32[]{:S(2)}, u32[]{:S(2)}) %collective-permute-start.4) | collective-permute-done | bytes 393248 | tf_op jit(solution)/shard_map/ppermute | solution.py:25
  150.5 1.5 fusion.40
  (492 shorter events, 19.2 us)
Async XLA Ops:
  78.7 2.1 %copy-start = (f32[4,3,64,128]{3,2,1,0:T(8,128)S(1)}, f32[4,3,64,128]{3,2,1,0:T(8,128)}, u32[]{:S(2)}) copy-start(f32[4,3,64,128]{3,2,1,0:T(8,128)} %param.9) | copy-start | bytes 1179652
  78.9 36.2 %collective-permute-start = (f32[4,3,64,128]{3,2,1,0:T(8,128)S(1)}, f32[4,3,64,128]{3,2,1,0:T(8,128)S(1)}, u32[]{:S(2)}, u32[]{:S(2)}) collective-permute-start(f32[4,3,64,128]{3,2,1,0:T(8,128)S(1)} %get-tuple-element.290), channel_id=1, source_target_pairs={{0,2},{2,4},{4,6},{6,8},{8,10},{10,12},{12,14},{14,16},{16,18},{18... | collective-permute-start | bytes 1179656 | tf_op jit(solution)/shard_map/ppermute | solution.py:25
  80.9 22.6 %collective-permute-start.7 = (f32[1,3,64,128]{3,2,1,0:T(8,128)S(1)}, f32[1,3,64,128]{3,2,1,0:T(8,128)S(1)}, u32[]{:S(2)}, u32[]{:S(2)}) collective-permute-start(f32[1,3,64,128]{3,2,1,0:T(8,128)S(1)} %get-tuple-element.303), channel_id=1, source_target_pairs={{0,2},{2,4},{4,6},{6,8},{8,10},{10,12},{12,14},{14,16},{16,18},{18... | collective-permute-start | bytes 294920 | tf_op jit(solution)/shard_map/ppermute | solution.py:36
  82.8 30.4 %collective-permute-start.6 = (f32[1,3,64,128]{3,2,1,0:T(8,128)S(1)}, f32[1,3,64,128]{3,2,1,0:T(8,128)S(1)}, u32[]{:S(2)}, u32[]{:S(2)}) collective-permute-start(f32[1,3,64,128]{3,2,1,0:T(8,128)S(1)} %get-tuple-element.302), channel_id=1, source_target_pairs={{2,0},{4,2},{6,4},{8,6},{10,8},{12,10},{14,12},{16,14},{18,16},{20... | collective-permute-start | bytes 294920 | tf_op jit(solution)/shard_map/ppermute | solution.py:37
  93.2 4.7 %collective-permute-start.8 = (f32[4,3,1,128]{3,2,1,0:T(1,128)S(1)}, f32[4,3,1,128]{3,2,1,0:T(1,128)S(1)}, u32[]{:S(2)}, u32[]{:S(2)}) collective-permute-start(f32[4,3,1,128]{3,2,1,0:T(1,128)S(1)} %get-tuple-element.300), channel_id=1, source_target_pairs={{1,0},{0,1},{3,2},{2,3},{5,4},{4,5},{7,6},{6,7},{9,8},{8,9},{11,10... | collective-permute-start | bytes 18440 | tf_op jit(solution)/shard_map/ppermute | solution.py:37
  95.8 5.8 %collective-permute-start.9 = (f32[4,3,1,128]{3,2,1,0:T(1,128)S(1)}, f32[4,3,1,128]{3,2,1,0:T(1,128)S(1)}, u32[]{:S(2)}, u32[]{:S(2)}) collective-permute-start(f32[4,3,1,128]{3,2,1,0:T(1,128)S(1)} %get-tuple-element.301), channel_id=1, source_target_pairs={{0,1},{1,0},{2,3},{3,2},{4,5},{5,4},{6,7},{7,6},{8,9},{9,8},{10,11... | collective-permute-start | bytes 18440 | tf_op jit(solution)/shard_map/ppermute | solution.py:36
  97.9 28.1 %collective-permute-start.1 = (f32[4,3,64,128]{3,2,1,0:T(8,128)S(1)}, f32[4,3,64,128]{3,2,1,0:T(8,128)S(1)}, u32[]{:S(2)}, u32[]{:S(2)}) collective-permute-start(f32[4,3,64,128]{3,2,1,0:T(8,128)S(1)} %get-tuple-element.295), channel_id=1, source_target_pairs={{0,510},{2,0},{4,2},{6,4},{8,6},{10,8},{12,10},{14,12},{16,14},{18... | collective-permute-start | bytes 1179656 | tf_op jit(solution)/shard_map/ppermute | solution.py:25
  101.6 28.8 %collective-permute-start.2 = (f32[4,3,64,128]{3,2,1,0:T(8,128)S(1)}, f32[4,3,64,128]{3,2,1,0:T(8,128)S(1)}, u32[]{:S(2)}, u32[]{:S(2)}) collective-permute-start(f32[4,3,64,128]{3,2,1,0:T(8,128)S(1)} %get-tuple-element.294), channel_id=1, source_target_pairs={{0,4},{2,6},{4,8},{6,10},{8,12},{10,14},{12,16},{14,18},{16,20},{1... | collective-permute-start | bytes 1179656 | tf_op jit(solution)/shard_map/ppermute | solution.py:25
  103.5 36.8 %collective-permute-start.3 = (f32[4,3,64,128]{3,2,1,0:T(8,128)S(1)}, f32[4,3,64,128]{3,2,1,0:T(8,128)S(1)}, u32[]{:S(2)}, u32[]{:S(2)}) collective-permute-start(f32[4,3,64,128]{3,2,1,0:T(8,128)S(1)} %get-tuple-element.293), channel_id=1, source_target_pairs={{0,508},{2,510},{4,0},{6,2},{8,4},{10,6},{12,8},{14,10},{16,12},{1... | collective-permute-start | bytes 1179656 | tf_op jit(solution)/shard_map/ppermute | solution.py:25
  113.2 37.3 %collective-permute-start.4 = (f32[4,3,64,128]{3,2,1,0:T(8,128)S(1)}, f32[4,3,64,128]{3,2,1,0:T(8,128)S(1)}, u32[]{:S(2)}, u32[]{:S(2)}) collective-permute-start(f32[4,3,64,128]{3,2,1,0:T(8,128)S(1)} %get-tuple-element.292), channel_id=1, source_target_pairs={{0,6},{2,8},{4,10},{6,12},{8,14},{10,16},{12,18},{14,20},{16,22},{... | collective-permute-start | bytes 1179656 | tf_op jit(solution)/shard_map/ppermute | solution.py:25
  115.2 35.4 %collective-permute-start.5 = (f32[4,3,64,128]{3,2,1,0:T(8,128)S(1)}, f32[4,3,64,128]{3,2,1,0:T(8,128)S(1)}, u32[]{:S(2)}, u32[]{:S(2)}) collective-permute-start(f32[4,3,64,128]{3,2,1,0:T(8,128)S(1)} %get-tuple-element.291), channel_id=1, source_target_pairs={{0,506},{2,508},{4,510},{6,0},{8,2},{10,4},{12,6},{14,8},{16,10},{... | collective-permute-start | bytes 1179656 | tf_op jit(solution)/shard_map/ppermute | solution.py:25
where the time goes:
time: 155 us; the launch traced here: 152 us
  starting transfers between devices  46.5 us (30%)
  matrix products  33.2 us (21%)
  other arithmetic  24.9 us (16%)
  waiting for transfers between devices  24.5 us (16%)
  blocking collectives  14.6 us (9%)
  loops' own time  4.07 us (3%)
  local copies, waits for them, and re-layouts  2.65 us (2%)
  between operations  1.56 us (1%)
    dot_general x32, matrix products, one_block(): lax.dot_general(scaled, y_weights, (((0,), (0,)), ((), ())), preferred_el...  33.2 us
    ppermute x6, starting transfers between devices, shifted(): lax.ppermute(x, axis, [(i, (i + by) % devices) for i in range(devices)])  29.7 us
    ppermute x6, waiting for transfers between devices, shifted(): lax.ppermute(x, axis, [(i, (i + by) % devices) for i in range(devices)])  24.5 us
    convert_element_type x32, other arithmetic, one_block(): scaled.reshape(block_size, band_depth * 3 * span_x).astype(jnp.bfloat16)  16 us
    ppermute x2, starting transfers between devices, with_halo(): lax.ppermute(leading, axis, [(b, a) for a, b in up])  13 us
    all_gather x1, blocking collectives, side_by_side(): filled, at, outs = (lax.all_gather(both, axis, axis=dim, tiled=True), 0, [])  8.47 us
    another operation x1, loops' own time, spread_band(): totals = lax.scan(one_block, totals, pieces)[0]  4.07 us
    ppermute x2, starting transfers between devices, with_halo(): lax.ppermute(last, axis, up)  3.84 us
  transfers between devices with their start and end apart: 10, of which 3 were waited for; matrix products, arithmetic and copies ran while one was open for 0% of the time, Pallas kernels for 0%

commit v1 on v0

v1 whole, which is shorter than its diff:
```python
import jax
import jax.numpy as jnp
from jax import lax
from jax.experimental import pallas as pl
from jax.experimental.pallas import tpu as pltpu
from jax.sharding import PartitionSpec as P

viscous = 0.15
ROWS = 32
ATTRS = 9
LIST = ROWS * ATTRS
KROWS = 4


def vmem():
    return pl.BlockSpec(memory_space=pltpu.VMEM)


def smem():
    return pl.BlockSpec(memory_space=pltpu.SMEM)


def corner_weights(t):
    q = jnp.sqrt(1.0 + 4.0 * t - 4.0 * t * t)
    return (
        (3.0 - 2.0 * t - q) / 8.0,
        (3.0 - 2.0 * t + q) / 8.0,
        (1.0 + 2.0 * t + q) / 8.0,
        (1.0 + 2.0 * t - q) / 8.0,
    )


def prepare(list_ref, base, first_plane, depth, span_x, span_y, span_z, rows_ref):
    def attr(a):
        return list_ref[pl.ds(base + a * ROWS, ROWS), :]

    def put(slot, value):
        rows_ref[pl.ds(slot * ROWS, ROWS), :] = value

    cx, cy = attr(6), attr(7)
    wx, wy, wz = corner_weights(attr(3)), corner_weights(attr(4)), corner_weights(attr(5))
    for b in range(4):
        tx, ty = cx + float(b), cy + float(b)
        put(b, jnp.where(tx >= float(span_x), tx - float(span_x), tx))
        put(4 + b, wx[b])
        put(8 + b, jnp.where(ty >= float(span_y), ty - float(span_y), ty))
        put(12 + b, wy[b].astype(jnp.bfloat16).astype(jnp.float32))
    rel = attr(8) - first_plane
    half = float(span_z // 2)
    rel = jnp.where(rel >= half, rel - float(span_z), rel)
    rel = jnp.where(rel < -half, rel + float(span_z), rel)
    for z in range(depth):
        plane = jnp.zeros_like(rel)
        for a in range(4):
            plane = jnp.where(rel == float(z - a), wz[a], plane)
        put(16 + z, plane)


def build(list_ref, base, rows_ref, row, depth, span_x, span_y, a_ref, b_ref):
    x_at = lax.broadcasted_iota(jnp.int32, (span_x, 128), 0).astype(jnp.float32)
    y_at = lax.broadcasted_iota(jnp.int32, (span_y, 128), 0).astype(jnp.float32)
    for r in range(KROWS):
        lanes = pl.ds(r * 128, 128)

        def get(slot):
            return rows_ref[pl.ds(slot * ROWS + row + r, 1), :]

        wx = jnp.zeros((span_x, 128), jnp.float32)
        wy = jnp.zeros((span_y, 128), jnp.float32)
        for b in range(4):
            wx = jnp.where(x_at == get(b), get(4 + b), wx)
            wy = jnp.where(y_at == get(8 + b), get(12 + b), wy)
        for c in range(3):
            force = list_ref[pl.ds(base + c * ROWS + row + r, 1), :]
            a_ref[pl.ds(c * span_x, span_x), lanes] = (wx * force).astype(jnp.bfloat16)
        for z in range(depth):
            b_ref[pl.ds(z * span_y, span_y), lanes] = (wy * get(16 + z)).astype(jnp.bfloat16)


def spread_list(list_ref, base, first_plane, acc_ref, dims, rows_ref, bufs):
    depth, span_x, span_y, span_z = dims
    turns = ROWS // KROWS
    prepare(list_ref, base, first_plane, depth, span_x, span_y, span_z, rows_ref)

    def fill(turn, which):
        build(list_ref, base, rows_ref, turn * KROWS, depth, span_x, span_y, *bufs[which])

    def add(which):
        a_ref, b_ref = bufs[which]
        out = lax.dot_general(
            a_ref[...], b_ref[...], (((1,), (1,)), ((), ())), preferred_element_type=jnp.float32
        )
        for z in range(depth):
            acc_ref[z] += out[:, z * span_y : (z + 1) * span_y]

    fill(0, 0)

    def two_turns(i, carry):
        fill(2 * i + 1, 1)
        add(0)
        fill(jnp.minimum(2 * i + 2, turns - 1), 0)
        add(1)
        return carry

    lax.fori_loop(0, turns // 2, two_turns, 0)


def scratch(dims):
    depth, span_x, span_y, _ = dims
    a = pltpu.VMEM((3 * span_x, KROWS * 128), jnp.bfloat16)
    b = pltpu.VMEM((depth * span_y, KROWS * 128), jnp.bfloat16)
    return [pltpu.VMEM((20 * ROWS, 128), jnp.float32), a, b, a, b]


def spread(markers, acc, plane, dims):
    depth, span_x, span_y, _ = dims
    lists = markers.shape[0] // LIST

    def kernel(*refs):
        if acc is None:
            plane_ref, list_ref, out_ref, rows_ref, a0, b0, a1, b1 = refs
            out_ref[...] = jnp.zeros_like(out_ref)
        else:
            plane_ref, list_ref, in_ref, out_ref, rows_ref, a0, b0, a1, b1 = refs
            out_ref[...] = in_ref[...]
        for n in range(lists):
            spread_list(list_ref, n * LIST, plane_ref[0], out_ref, dims, rows_ref, ((a0, b0), (a1, b1)))

    operands = (plane, markers) if acc is None else (plane, markers, acc)
    return pl.pallas_call(
        kernel,
        out_shape=jax.ShapeDtypeStruct((depth, 3 * span_x, span_y), jnp.float32),
        in_specs=[smem()] + [vmem()] * (len(operands) - 1),
        out_specs=vmem(),
        scratch_shapes=scratch(dims),
        cost_estimate=pl.CostEstimate(
            flops=lists * 4096 * 3 * span_x * depth * span_y * 2, bytes_accessed=2000000, transcendentals=0
        ),
        name="spread",
    )(*operands)


def by_core(x, gz_count, by):
    pairs = []
    for g in range(gz_count):
        pairs.append((2 * g, 2 * ((g + by) % gz_count)))
        pairs.append((2 * g + 1, 2 * ((g - by) % gz_count) + 1))
    return lax.ppermute(x, ("gz", "col"), pairs)


def on_device(velocity, forces, offsets, cell_x, cell_y, cell_z, band_start):
    depth, _, half_x, span_y = velocity.shape
    gz_count = lax.axis_size("gz")
    gz_index = lax.axis_index("gz")
    col = lax.axis_index("col")
    span_x = half_x * lax.axis_size("col")
    dims = (depth, span_x, span_y, gz_count * depth)
    z_base = (band_start[0] * depth + cell_z).astype(jnp.float32)
    markers = jnp.concatenate(
        [
            forces.reshape(3 * ROWS, 128),
            offsets.reshape(3 * ROWS, 128),
            cell_x.astype(jnp.float32).reshape(ROWS, 128),
            cell_y.astype(jnp.float32).reshape(ROWS, 128),
            z_base.reshape(ROWS, 128),
        ]
    )
    plane_rows = 3 * half_x
    first, last = velocity[0].reshape(plane_rows, span_y), velocity[-1].reshape(plane_rows, span_y)
    mine_out = jnp.where(col == 0, last, first)
    other_out = jnp.where(col == 0, first, last)
    x_low = velocity[:, :, 0].reshape(3 * depth, span_y)
    x_high = velocity[:, :, -1].reshape(3 * depth, span_y)
    sent = jnp.concatenate([markers, other_out, x_low, x_high])
    both = lax.all_gather(sent, "col", axis=0, tiled=False)
    chip = both[:, :LIST].reshape(2 * LIST, 128)
    partner = lax.dynamic_index_in_dim(both[:, LIST:], 1 - col, 0, keepdims=False)
    plane_out = jnp.concatenate([mine_out, partner[:plane_rows]])
    partner_low = partner[plane_rows : plane_rows + 3 * depth].reshape(depth, 3, 1, span_y)
    partner_high = partner[plane_rows + 3 * depth :].reshape(depth, 3, 1, span_y)

    second = by_core(chip, gz_count, 2)
    nearest = by_core(jnp.concatenate([chip, plane_out]), gz_count, 1)
    third = by_core(second, gz_count, 1)

    slab = (gz_index * depth).astype(jnp.float32).reshape(1)
    acc = spread(markers, None, slab, dims)
    acc = spread(second, acc, slab, dims)
    acc = spread(nearest[: 2 * LIST], acc, slab, dims)
    acc = spread(third, acc, slab, dims)
    acc = acc.reshape(depth, 3, span_x, span_y)

    keep = lax.dynamic_slice_in_dim(acc, col * half_x, half_x, 2)
    give = lax.dynamic_slice_in_dim(acc, (1 - col) * half_x, half_x, 2)
    my_plane = nearest[2 * LIST : 2 * LIST + plane_rows]
    its_plane = nearest[2 * LIST + plane_rows :]
    swapped = lax.ppermute(
        jnp.concatenate([give.reshape(-1, span_y), its_plane]), "col", [(0, 1), (1, 0)]
    )
    force = keep + swapped[: depth * plane_rows].reshape(keep.shape)
    got_plane = swapped[depth * plane_rows :]
    below = jnp.where(col == 0, my_plane, got_plane).reshape(1, 3, half_x, span_y)
    above = jnp.where(col == 0, got_plane, my_plane).reshape(1, 3, half_x, span_y)
    padded = jnp.concatenate([below, velocity, above])
    across = jnp.concatenate([partner_high, velocity, partner_low], axis=2)
    neighbours = padded[2:] + padded[:-2] + across[:, :, 2:] + across[:, :, :-2]
    neighbours = neighbours + jnp.roll(velocity, 1, 3) + jnp.roll(velocity, -1, 3)
    velocity_next = velocity + viscous * (neighbours - 6.0 * velocity) + force
    return (force, velocity_next)


def solution(mesh):
    in_specs = (
        P("gz", None, "col", None),
        P(None, ("gz", "col")),
        P(None, ("gz", "col")),
        P(("gz", "col")),
        P(("gz", "col")),
        P(("gz", "col")),
        P("gz"),
    )
    out_specs = (P("gz", None, "col", None), P("gz", None, "col", None))
    return jax.shard_map(
        on_device, mesh=mesh, in_specs=in_specs, out_specs=out_specs, check_vma=False
    )
```

time: 155 us -> 79.3 us (0.51); the launches traced: 152 us -> 78.5 us
  Pallas kernels: 0 us -> 36.2 us
  matrix products: 33.2 us -> 0 us
  starting transfers between devices: 46.5 us -> 20.2 us
  waiting for transfers between devices: 24.5 us -> 1.46 us
  other arithmetic: 24.9 us -> 2.14 us
  blocking collectives: 14.6 us -> 8.63 us
  local copies, waits for them, and re-layouts: 2.65 us -> 8.39 us
  loops' own time: 4.07 us -> 0 us
    pallas_call x0 -> x4, Pallas kernels: none -> 36.2 us  [spread(): pl.pallas_call(kernel, out_shape=jax.ShapeDtypeStruct((depth, 3 * span_x,...]
    dot_general x32 -> x0, matrix products: 33.2 us -> none  [one_block(): lax.dot_general(scaled, y_weights, (((0,), (0,)), ((), ())), preferred_el...]
    ppermute x10 -> x4, starting transfers between devices: 46.5 us -> 20.2 us  [the longest x3 18.3 us: by_core(): return lax.ppermute(x, ('gz', 'col'), pairs)]
    ppermute x10 -> x4, waiting for transfers between devices: 24.5 us -> 1.46 us  [the longest x1 1.45 us: on_device(): lax.ppermute(jnp.concatenate([give.reshape(-1, span_y), its_plane]), 'col...]
    convert_element_type x32 -> x0, other arithmetic: 16 us -> none  [one_block(): scaled.reshape(block_size, band_depth * 3 * span_x).astype(jnp.bfloat16)]
    all_gather x4 -> x1, blocking collectives: 14.6 us -> 8.63 us  [on_device(): both = lax.all_gather(sent, 'col', axis=0, tiled=False)]
    another operation x1 -> x0, loops' own time: 4.07 us -> none  [spread_band(): totals = lax.scan(one_block, totals, pieces)[0]]
    add x97 -> x1, other arithmetic: 5.14 us -> 1.28 us  [on_device(): velocity_next = velocity + viscous * (neighbours - 6.0 * velocity) + force]
  transfers between devices with their start and end apart: 10 -> 4, of which waited for: 3 -> 1; matrix products, arithmetic and copies ran while one was open for 0% -> 2% of each run, Pallas kernels for 0% -> 33%
where the time goes in v1:
time: 79.3 us; the launch traced here: 78.5 us
  Pallas kernels  36.2 us (46%)
  starting transfers between devices  20.2 us (25%)
  blocking collectives  8.63 us (11%)
  local copies, waits for them, and re-layouts  8.39 us (11%)
  other arithmetic  2.14 us (3%)
  between operations  1.53 us (2%)
  waiting for transfers between devices  1.46 us (2%)
    pallas_call x4, Pallas kernels, spread(): pl.pallas_call(kernel, out_shape=jax.ShapeDtypeStruct((depth, 3 * span_x,...  36.2 us
    ppermute x3, starting transfers between devices, by_core(): return lax.ppermute(x, ('gz', 'col'), pairs)  18.3 us
    all_gather x1, blocking collectives, on_device(): both = lax.all_gather(sent, 'col', axis=0, tiled=False)  8.63 us
    unnamed x18, local copies, waits for them, and re-layouts  3.35 us
    ppermute x1, starting transfers between devices, on_device(): lax.ppermute(jnp.concatenate([give.reshape(-1, span_y), its_plane]), 'col...  1.92 us
  transfers between devices with their start and end apart: 4, of which 1 were waited for; matrix products, arithmetic and copies ran while one was open for 2% of the time, Pallas kernels for 33%

profile of v1, /device:TPU:1, one launch (start us, length us, event | category | flops | bytes accessed | tf_op | source)
XLA Modules:
  0.0 78.5 jit_solution(13711722414579872433)
XLA Ops:
  0.6 0.0 copy-start
  1.3 0.9 %slice_reduce_fusion = (f32[4,3,128]{2,1,0:T(4,128)S(1)}, f32[4,3,128]{2,1,0:T(4,128)S(1)}) fusion(f32[4,3,64,128]{3,2,1,0:T(8,128)} %param.7), kind=kLoop, calls=%fused_computation.29 | loop fusion | bytes 24576 | tf_op jit(solution)/shard_map/slice | solution.py:173
  2.2 0.9 %reshape.58 = f32[96,128]{1,0:T(8,128)S(1)} reshape(f32[3,4096]{1,0:T(4,128)} %param.8) | data formatting | bytes 98304 | tf_op jit(solution)/shard_map/reshape | solution.py:161
  3.1 0.9 %reshape.59 = f32[96,128]{1,0:T(8,128)S(1)} reshape(f32[3,4096]{1,0:T(4,128)} %param.9) | data formatting | bytes 98304 | tf_op jit(solution)/shard_map/reshape | solution.py:162
  4.0 0.7 convert_bitcast_fusion.1
  4.8 0.0 copy-start.2
  4.8 0.7 copy-done.2
  5.5 0.0 copy-start.3
  5.5 0.7 copy-done.3
  6.2 0.0 copy-done
  6.2 0.0 copy-start.4
  6.2 0.7 copy-done.4
  6.9 0.0 copy-start.5
  6.9 0.1 concatenate.35
  7.1 0.5 copy-done.5
  7.6 8.6 %all-gather = f32[1008,128]{1,0:T(8,128)S(1)} all-gather(f32[504,128]{1,0:T(8,128)S(1)} %concatenate.35), channel_id=2, replica_groups=mesh['gz'=256,'col'=2] {'col'}, dimensions={0}, use_global_device_ids=true | all-gather | bytes 774144 | tf_op jit(solution)/shard_map/all_gather | solution.py:175
  16.2 11.2 %collective-permute-start = (f32[576,128]{1,0:T(8,128)S(1)}, f32[576,128]{1,0:T(8,128)S(1)}, u32[]{:S(2)}, u32[]{:S(2)}) collective-permute-start(f32[576,128]{1,0:T(8,128)S(1)} %bitcast.28), channel_id=1, source_target_pairs={{0,4},{1,509},{2,6},{3,511},{4,8},{5,1},{6,10},{7,3},{8,12},{9,5},... | collective-permute-start | bytes 884744 | tf_op jit(solution)/shard_map/ppermute | solution.py:148
  27.5 3.0 %collective-permute-start.2 = (f32[960,128]{1,0:T(8,128)S(1)}, f32[960,128]{1,0:T(8,128)S(1)}, u32[]{:S(2)}, u32[]{:S(2)}) collective-permute-start(f32[960,128]{1,0:T(8,128)S(1)} %pad_maximum_fusion), channel_id=1, source_target_pairs={{0,2},{1,511},{2,4},{3,1},{4,6},{5,3},{6,8},{7,5},{8,10},{9,7},{10... | collective-permute-start | bytes 1474568 | tf_op jit(solution)/shard_map/ppermute | solution.py:148
  30.6 5.8 %spread.4.refs_2_ = f32[4,384,128]{2,1,0:T(8,128)} custom-call(f32[1]{0:T(128)} %bitcast.refs_0_, f32[288,128]{1,0:T(8,128)} %copy-done.5), custom_call_target="tpu_custom_call" | custom-call | flops 1610612736 | bytes 2000000 | tf_op jit(solution)/shard_map/spread/pallas_call | solution.py:130
  36.4 0.0 collective-permute-done.refs_1_
  36.4 0.0 copy-start.6
  36.4 4.1 %collective-permute-start.1 = (f32[576,128]{1,0:T(8,128)S(1)}, f32[576,128]{1,0:T(8,128)S(1)}, u32[]{:S(2)}, u32[]{:S(2)}) collective-permute-start(f32[576,128]{1,0:T(8,128)S(1)} %collective-permute-done.refs_1_), channel_id=1, source_target_pairs={{0,2},{1,511},{2,4},{3,1},{4,6},{5,3},{6,8},{7,5},{8,10},{9,7},{10... | collective-permute-start | bytes 884744 | tf_op jit(solution)/shard_map/ppermute | solution.py:148
  40.6 0.0 copy-done.6
  40.6 10.1 %spread.5.refs_2_ = f32[4,384,128]{2,1,0:T(8,128)} custom-call(f32[1]{0:T(128)} %bitcast.refs_0_, f32[576,128]{1,0:T(8,128)} %copy-done.6, f32[4,384,128]{2,1,0:T(8,128)} %spread.4.refs_2_), custom_call_target="tpu_custom_call" | custom-call | flops 3221225472 | bytes 2000000 | tf_op jit(solution)/shard_map/spread/pallas_call | solution.py:130
  50.7 0.0 collective-permute-done.2
  50.7 0.7 slice.104.refs_1_
  51.4 10.1 %spread.6.refs_2_ = f32[4,384,128]{2,1,0:T(8,128)} custom-call(f32[1]{0:T(128)} %bitcast.refs_0_, f32[576,128]{1,0:T(8,128)} %slice.104.refs_1_, f32[4,384,128]{2,1,0:T(8,128)} %spread.5.refs_2_), custom_call_target="tpu_custom_call" | custom-call | flops 3221225472 | bytes 2000000 | tf_op jit(solution)/shard_map/spread/pallas_call | solution.py:130
  61.5 0.0 collective-permute-done.1.refs_1_
  61.5 0.0 copy-start.7
  61.5 0.7 copy-done.7
  62.2 10.1 %spread.7 = f32[4,384,128]{2,1,0:T(8,128)} custom-call(f32[1]{0:T(128)} %bitcast.refs_0_, f32[576,128]{1,0:T(8,128)} %copy-done.7, f32[4,384,128]{2,1,0:T(8,128)} %spread.6.refs_2_), custom_call_target="tpu_custom_call" | custom-call | flops 3221225472 | bytes 2000000 | tf_op jit(solution)/shard_map/spread/pallas_call | solution.py:130
  72.3 1.0 %constant_dynamic-slice_fusion.1 = f32[4,3,64,128]{3,2,1,0:T(8,128)S(1)} fusion(f32[4,3,128,128]{3,2,1,0:T(8,128)} %bitcast.30, s32[]{:T(128)S(6)} %select_n.45), kind=kLoop, calls=%fused_computation.32 | loop fusion | bytes 786436 | tf_op jit(solution)/shard_map/dynamic_slice | solution.py:194
  73.4 1.9 %collective-permute-start.3 = (f32[960,128]{1,0:T(8,128)S(1)}, f32[960,128]{1,0:T(8,128)S(1)}, u32[]{:S(2)}, u32[]{:S(2)}) collective-permute-start(f32[960,128]{1,0:T(8,128)S(1)} %pad_maximum_fusion.1), channel_id=1, source_target_pairs={{0,1},{1,0},{2,3},{3,2},{4,5},{5,4},{6,7},{7,6},{8,9},{9,8},{10,11... | collective-permute-start | bytes 1474568 | tf_op jit(solution)/shard_map/ppermute | solution.py:197
  75.3 0.2 fusion.10
  75.5 0.2 fusion.9
  75.7 0.0 copy-start.1
  75.7 1.5 %collective-permute-done.3 = f32[960,128]{1,0:T(8,128)S(1)} collective-permute-done((f32[960,128]{1,0:T(8,128)S(1)}, f32[960,128]{1,0:T(8,128)S(1)}, u32[]{:S(2)}, u32[]{:S(2)}) %collective-permute-start.3) | collective-permute-done | bytes 491552 | tf_op jit(solution)/shard_map/ppermute | solution.py:197
  77.2 0.0 copy-done.1
  77.2 1.3 %fusion.6 = (f32[4,3,64,128]{3,2,1,0:T(8,128)}, f32[4,3,64,128]{3,2,1,0:T(8,128)}) fusion(f32[4,3,64,128]{3,2,1,0:T(8,128)S(1)} %copy-done, f32[4,3,1,128]{3,2,1,0:T(1,128)S(1)} %reshape.70, f32[4,3,1,128]{3,2,1,0:T(1,128)S(1)} %reshape.69, f32[1,3,64,128]{3,2,1,0:T(8,128)S(1)} %bitcast.35, f32[1,3,64,128]{3,2,1,0:T(8,128)S(1)} %bitcast.34, ...), kind=kLoop, calls=%fused_computation.9 | loop fusion | flops 1671168 | bytes 2961412 | tf_op jit(solution)/shard_map/add | solution.py:208
  (19 shorter events, 0.3 us)
Async XLA Ops:
  0.6 5.6 %copy-start = (f32[4,3,64,128]{3,2,1,0:T(8,128)S(1)}, f32[4,3,64,128]{3,2,1,0:T(8,128)}, u32[]{:S(2)}) copy-start(f32[4,3,64,128]{3,2,1,0:T(8,128)} %param.7) | copy-start | bytes 1179652
  4.8 0.7 copy-start.2
  5.5 0.7 copy-start.3
  6.2 0.7 copy-start.4
  6.9 0.7 copy-start.5
  16.2 20.2 %collective-permute-start = (f32[576,128]{1,0:T(8,128)S(1)}, f32[576,128]{1,0:T(8,128)S(1)}, u32[]{:S(2)}, u32[]{:S(2)}) collective-permute-start(f32[576,128]{1,0:T(8,128)S(1)} %bitcast.28), channel_id=1, source_target_pairs={{0,4},{1,509},{2,6},{3,511},{4,8},{5,1},{6,10},{7,3},{8,12},{9,5},... | collective-permute-start | bytes 884744 | tf_op jit(solution)/shard_map/ppermute | solution.py:148
  27.5 23.1 %collective-permute-start.2 = (f32[960,128]{1,0:T(8,128)S(1)}, f32[960,128]{1,0:T(8,128)S(1)}, u32[]{:S(2)}, u32[]{:S(2)}) collective-permute-start(f32[960,128]{1,0:T(8,128)S(1)} %pad_maximum_fusion), channel_id=1, source_target_pairs={{0,2},{1,511},{2,4},{3,1},{4,6},{5,3},{6,8},{7,5},{8,10},{9,7},{10... | collective-permute-start | bytes 1474568 | tf_op jit(solution)/shard_map/ppermute | solution.py:148
  36.4 4.1 %copy-start.6 = (f32[576,128]{1,0:T(8,128)}, f32[576,128]{1,0:T(8,128)S(1)}, u32[]{:S(2)}) copy-start(f32[576,128]{1,0:T(8,128)S(1)} %collective-permute-done.refs_1_) | copy-start | bytes 884740
  36.4 25.1 %collective-permute-start.1 = (f32[576,128]{1,0:T(8,128)S(1)}, f32[576,128]{1,0:T(8,128)S(1)}, u32[]{:S(2)}, u32[]{:S(2)}) collective-permute-start(f32[576,128]{1,0:T(8,128)S(1)} %collective-permute-done.refs_1_), channel_id=1, source_target_pairs={{0,2},{1,511},{2,4},{3,1},{4,6},{5,3},{6,8},{7,5},{8,10},{9,7},{10... | collective-permute-start | bytes 884744 | tf_op jit(solution)/shard_map/ppermute | solution.py:148
  61.5 0.7 copy-start.7
  73.4 3.8 %collective-permute-start.3 = (f32[960,128]{1,0:T(8,128)S(1)}, f32[960,128]{1,0:T(8,128)S(1)}, u32[]{:S(2)}, u32[]{:S(2)}) collective-permute-start(f32[960,128]{1,0:T(8,128)S(1)} %pad_maximum_fusion.1), channel_id=1, source_target_pairs={{0,1},{1,0},{2,3},{3,2},{4,5},{5,4},{6,7},{7,6},{8,9},{9,8},{10,11... | collective-permute-start | bytes 1474568 | tf_op jit(solution)/shard_map/ppermute | solution.py:197
  75.7 1.5 %copy-start.1 = (f32[4,384,128]{2,1,0:T(8,128)S(1)}, f32[4,384,128]{2,1,0:T(8,128)}, u32[]{:S(2)}) copy-start(f32[4,384,128]{2,1,0:T(8,128)} %spread.7) | copy-start | bytes 2359300

commit v2 on v1

v2 whole, which is shorter than its diff:
```python
import jax
import jax.numpy as jnp
from jax import lax
from jax.experimental import pallas as pl
from jax.experimental.pallas import tpu as pltpu
from jax.sharding import PartitionSpec as P

viscous = 0.15
ROWS = 32
ATTRS = 9
LIST = ROWS * ATTRS
KROWS = 8
SLOTS = 24
TILE = 16


def vmem():
    return pl.BlockSpec(memory_space=pltpu.VMEM)


def smem():
    return pl.BlockSpec(memory_space=pltpu.SMEM)


def corner_weights(t):
    q = jnp.sqrt(1.0 + 4.0 * t - 4.0 * t * t)
    return (
        (3.0 - 2.0 * t - q) / 8.0,
        (3.0 - 2.0 * t + q) / 8.0,
        (1.0 + 2.0 * t + q) / 8.0,
        (1.0 + 2.0 * t - q) / 8.0,
    )


def in_vmem(x):
    return pltpu.with_memory_space_constraint(x, pltpu.VMEM)


def prepare(list_ref, n, first_plane, dims, rows_ref):
    depth, span_x, span_y, span_z = dims

    def attr(a):
        return list_ref[pl.ds(n * LIST + a * ROWS, ROWS), :]

    def put(slot, value):
        rows_ref[pl.ds((n * SLOTS + slot) * ROWS, ROWS), :] = value

    def along(slot, cell, weights, span):
        tile = jnp.floor(cell * (1.0 / TILE))
        low = cell - tile * float(TILE)
        for b in range(4):
            at = low + float(b)
            put(slot + b, jnp.where(at >= float(TILE), at - float(TILE), at))
            put(slot + 4 + b, weights[b])
        put(slot + 8, tile)
        put(slot + 9, jnp.where(tile >= float(span // TILE - 1), 0.0, tile + 1.0))

    along(0, attr(6), corner_weights(attr(3)), span_x)
    rounded = [w.astype(jnp.bfloat16).astype(jnp.float32) for w in corner_weights(attr(4))]
    along(10, attr(7), rounded, span_y)
    wz = corner_weights(attr(5))
    rel = attr(8) - first_plane
    half = float(span_z // 2)
    rel = jnp.where(rel >= half, rel - float(span_z), rel)
    rel = jnp.where(rel < -half, rel + float(span_z), rel)
    for z in range(depth):
        plane = jnp.zeros_like(rel)
        for a in range(4):
            plane = jnp.where(rel == float(z - a), wz[a], plane)
        put(20 + z, plane)


def build(list_ref, rows_ref, turn, dims, a_ref, b_ref):
    depth, span_x, span_y, _ = dims
    per_list = ROWS // KROWS
    n = turn // per_list
    row = (turn % per_list) * KROWS
    row_at = lax.broadcasted_iota(jnp.int32, (TILE, 128), 0).astype(jnp.float32)
    nothing = jnp.zeros((TILE, 128), jnp.bfloat16)
    for r in range(KROWS):
        lanes = pl.ds(r * 128, 128)

        def get(slot):
            return rows_ref[pl.ds((n * SLOTS + slot) * ROWS + row + r, 1), :]

        def pattern(slot):
            weights = jnp.zeros((TILE, 128), jnp.float32)
            for b in range(4):
                weights = jnp.where(row_at == get(slot + b), get(slot + 4 + b), weights)
            tiles = jnp.where(row_at >= get(slot), get(slot + 8), get(slot + 9))
            return weights, tiles.astype(jnp.bfloat16)

        wx, x_tile = pattern(0)
        forces = [list_ref[pl.ds(n * LIST + c * ROWS + row + r, 1), :] for c in range(3)]
        a_rows = [(wx * f).astype(jnp.bfloat16) for f in forces]
        for t in range(span_x // TILE):
            here = x_tile == jnp.bfloat16(t)
            for c in range(3):
                a_ref[pl.ds(c * span_x + t * TILE, TILE), lanes] = jnp.where(here, a_rows[c], nothing)
        wy, y_tile = pattern(10)
        b_rows = [(wy * get(20 + z)).astype(jnp.bfloat16) for z in range(depth)]
        for t in range(span_y // TILE):
            here = y_tile == jnp.bfloat16(t)
            for z in range(depth):
                b_ref[pl.ds(z * span_y + t * TILE, TILE), lanes] = jnp.where(here, b_rows[z], nothing)


def spread_lists(list_ref, lists, first_plane, acc_ref, dims, rows_ref, bufs):
    depth, span_x, span_y, _ = dims
    turns = lists * (ROWS // KROWS)
    for n in range(lists):
        prepare(list_ref, n, first_plane, dims, rows_ref)

    def fill(turn, which):
        build(list_ref, rows_ref, turn, dims, *bufs[which])

    def add(which):
        a_ref, b_ref = bufs[which]
        out = lax.dot_general(
            a_ref[...], b_ref[...], (((1,), (1,)), ((), ())), preferred_element_type=jnp.float32
        )
        for z in range(depth):
            acc_ref[z] += out[:, z * span_y : (z + 1) * span_y]

    fill(0, 0)

    def two_turns(i, carry):
        fill(2 * i + 1, 1)
        add(0)
        fill(jnp.minimum(2 * i + 2, turns - 1), 0)
        add(1)
        return carry

    lax.fori_loop(0, turns // 2, two_turns, 0)


def scratch(lists, dims):
    depth, span_x, span_y, _ = dims
    a = pltpu.VMEM((3 * span_x, KROWS * 128), jnp.bfloat16)
    b = pltpu.VMEM((depth * span_y, KROWS * 128), jnp.bfloat16)
    return [pltpu.VMEM((lists * SLOTS * ROWS, 128), jnp.float32), a, b, a, b]


def cost(lists, dims):
    depth, span_x, span_y, _ = dims
    return pl.CostEstimate(
        flops=lists * ROWS * 128 * 3 * span_x * depth * span_y * 2,
        bytes_accessed=2000000,
        transcendentals=0,
    )


def spread(markers, lists, acc, plane, dims):
    depth, span_x, span_y, _ = dims

    def kernel(*refs):
        if acc is None:
            plane_ref, list_ref, out_ref, rows_ref, a0, b0, a1, b1 = refs
            out_ref[...] = jnp.zeros_like(out_ref)
        else:
            plane_ref, list_ref, _, out_ref, rows_ref, a0, b0, a1, b1 = refs
        spread_lists(list_ref, lists, plane_ref[0], out_ref, dims, rows_ref, ((a0, b0), (a1, b1)))

    operands = (plane, in_vmem(markers))
    if acc is not None:
        operands += (in_vmem(acc),)
    return pl.pallas_call(
        kernel,
        out_shape=pltpu.VMEM((depth, 3 * span_x, span_y), jnp.float32),
        in_specs=[smem()] + [vmem()] * (len(operands) - 1),
        out_specs=vmem(),
        input_output_aliases={} if acc is None else {2: 0},
        scratch_shapes=scratch(lists, dims),
        cost_estimate=cost(lists, dims),
        name="spread",
    )(*operands)


def spread_last(markers, lists, acc, nearest, plane, col, dims):
    depth, span_x, span_y, _ = dims
    half = span_x // 2
    rows = depth * 3 * half
    plane_at = 2 * LIST + 3 * half

    def kernel(plane_ref, col_ref, list_ref, in_ref, near_ref, keep_ref, give_ref, acc_ref, rows_ref, a0, b0, a1, b1):
        acc_ref[...] = in_ref[...]
        give_ref[pl.ds(rows, 3 * half), :] = near_ref[pl.ds(plane_at, 3 * half), :]
        spread_lists(list_ref, lists, plane_ref[0], acc_ref, dims, rows_ref, ((a0, b0), (a1, b1)))
        mine = pl.multiple_of(col_ref[0] * half, half)
        other = pl.multiple_of((1 - col_ref[0]) * half, half)
        for z in range(depth):
            for c in range(3):
                at = pl.ds((z * 3 + c) * half, half)
                keep_ref[at, :] = acc_ref[z, pl.ds(c * span_x + mine, half), :]
                give_ref[at, :] = acc_ref[z, pl.ds(c * span_x + other, half), :]

    return pl.pallas_call(
        kernel,
        out_shape=(
            pltpu.VMEM((rows, span_y), jnp.float32),
            pltpu.VMEM((rows + 3 * half, span_y), jnp.float32),
        ),
        in_specs=[smem(), smem(), vmem(), vmem(), vmem()],
        out_specs=(vmem(), vmem()),
        scratch_shapes=[pltpu.VMEM((depth, 3 * span_x, span_y), jnp.float32)] + scratch(lists, dims),
        cost_estimate=cost(lists, dims),
        name="spread_last",
    )(plane, col, in_vmem(markers), in_vmem(acc), in_vmem(nearest))


def pack(velocity, forces, offsets, cell_x, cell_y, cell_z, band_start, col):
    depth, _, half, span_y = velocity.shape
    plane_rows = 3 * half
    total = LIST + plane_rows + 6 * depth

    def kernel(col_ref, start_ref, v_ref, f_ref, o_ref, x_ref, y_ref, z_ref, sent_ref, plane_ref):
        for k in range(ROWS):
            for c in range(3):
                sent_ref[pl.ds(c * ROWS + k, 1), :] = f_ref[pl.ds(c, 1), pl.ds(k * 128, 128)]
                sent_ref[pl.ds((3 + c) * ROWS + k, 1), :] = o_ref[pl.ds(c, 1), pl.ds(k * 128, 128)]
        sent_ref[pl.ds(6 * ROWS, ROWS), :] = x_ref[...].astype(jnp.float32)
        sent_ref[pl.ds(7 * ROWS, ROWS), :] = y_ref[...].astype(jnp.float32)
        sent_ref[pl.ds(8 * ROWS, ROWS), :] = (z_ref[...] + start_ref[0] * depth).astype(jnp.float32)
        to_core = jnp.where(col_ref[0] == 0, 0, depth - 1)
        for c in range(3):
            sent_ref[pl.ds(LIST + c * half, half), :] = v_ref[to_core, c]
            plane_ref[pl.ds(c * half, half), :] = v_ref[depth - 1 - to_core, c]
        for z in range(depth):
            for c in range(3):
                at = LIST + plane_rows + z * 3 + c
                sent_ref[pl.ds(at, 1), :] = v_ref[z, c, pl.ds(0, 1), :]
                sent_ref[pl.ds(at + 3 * depth, 1), :] = v_ref[z, c, pl.ds(half - 1, 1), :]

    return pl.pallas_call(
        kernel,
        out_shape=(
            pltpu.VMEM((total, span_y), jnp.float32),
            pltpu.VMEM((plane_rows, span_y), jnp.float32),
        ),
        in_specs=[smem(), smem()] + [vmem()] * 6,
        out_specs=(vmem(), vmem()),
        name="pack",
    )(
        col,
        band_start,
        velocity,
        forces,
        offsets,
        cell_x.reshape(ROWS, 128),
        cell_y.reshape(ROWS, 128),
        cell_z.reshape(ROWS, 128),
    )


def by_core(x, gz_count, by):
    pairs = []
    for g in range(gz_count):
        pairs.append((2 * g, 2 * ((g + by) % gz_count)))
        pairs.append((2 * g + 1, 2 * ((g - by) % gz_count) + 1))
    return lax.ppermute(x, ("gz", "col"), pairs)


def on_device(velocity, forces, offsets, cell_x, cell_y, cell_z, band_start):
    depth, _, half_x, span_y = velocity.shape
    gz_count = lax.axis_size("gz")
    gz_index = lax.axis_index("gz")
    col = lax.axis_index("col")
    span_x = half_x * lax.axis_size("col")
    dims = (depth, span_x, span_y, gz_count * depth)
    core = col.reshape(1)
    plane_rows = 3 * half_x
    sent, mine_out = pack(velocity, forces, offsets, cell_x, cell_y, cell_z, band_start, core)
    both = lax.all_gather(sent, "col", axis=0, tiled=False)
    chip = both[:, :LIST].reshape(2 * LIST, 128)
    partner = lax.dynamic_index_in_dim(both[:, LIST:], 1 - col, 0, keepdims=False)
    plane_out = jnp.concatenate([mine_out, partner[:plane_rows]])
    partner_low = partner[plane_rows : plane_rows + 3 * depth].reshape(depth, 3, 1, span_y)
    partner_high = partner[plane_rows + 3 * depth :].reshape(depth, 3, 1, span_y)

    second = by_core(chip, gz_count, 2)
    nearest = by_core(jnp.concatenate([chip, plane_out]), gz_count, 1)
    third = by_core(second, gz_count, 1)

    slab = (gz_index * depth).astype(jnp.float32).reshape(1)
    acc = spread(sent, 1, None, slab, dims)
    acc = spread(second, 2, acc, slab, dims)
    acc = spread(nearest, 2, acc, slab, dims)
    keep, give = spread_last(third, 2, acc, nearest, slab, core, dims)
    my_plane = nearest[2 * LIST : 2 * LIST + plane_rows]
    swapped = lax.ppermute(give, "col", [(0, 1), (1, 0)])
    keep = keep.reshape(depth, 3, half_x, span_y)
    force = keep + swapped[: depth * plane_rows].reshape(keep.shape)
    got_plane = swapped[depth * plane_rows :]
    below = jnp.where(col == 0, my_plane, got_plane).reshape(1, 3, half_x, span_y)
    above = jnp.where(col == 0, got_plane, my_plane).reshape(1, 3, half_x, span_y)
    padded = jnp.concatenate([below, velocity, above])
    across = jnp.concatenate([partner_high, velocity, partner_low], axis=2)
    neighbours = padded[2:] + padded[:-2] + across[:, :, 2:] + across[:, :, :-2]
    neighbours = neighbours + jnp.roll(velocity, 1, 3) + jnp.roll(velocity, -1, 3)
    velocity_next = velocity + viscous * (neighbours - 6.0 * velocity) + force
    return (force, velocity_next)


def solution(mesh):
    in_specs = (
        P("gz", None, "col", None),
        P(None, ("gz", "col")),
        P(None, ("gz", "col")),
        P(("gz", "col")),
        P(("gz", "col")),
        P(("gz", "col")),
        P("gz"),
    )
    out_specs = (P("gz", None, "col", None), P("gz", None, "col", None))
    return jax.shard_map(
        on_device, mesh=mesh, in_specs=in_specs, out_specs=out_specs, check_vma=False
    )
```

time: 79.3 us -> 56.2 us (0.71)
  Pallas kernels: 36.2 us -> 19.5 us
  local copies, waits for them, and re-layouts: 8.39 us -> 0.47 us
  starting transfers between devices: 20.2 us -> 22.3 us
  other arithmetic: 2.14 us -> 1.23 us
  waiting for transfers between devices: 1.46 us -> 2.3 us
    pallas_call x4 -> x5, Pallas kernels: 36.2 us -> 19.5 us  [the longest x3 13.1 us: spread(): pl.pallas_call(kernel, out_shape=pltpu.VMEM((depth, 3 * span_x, span_y),...]
    unnamed x18 -> x4, local copies, waits for them, and re-layouts: 3.35 us -> 0.01 us
    ppermute x3, starting transfers between devices: 18.3 us -> 20.4 us  [by_core(): return lax.ppermute(x, ('gz', 'col'), pairs)]
    reshape x2 -> x0, local copies, waits for them, and re-layouts: 1.76 us -> none  [the longest x1 0.88 us: on_device(): forces.reshape(3 * ROWS, 128)]
    slice x4 -> x0, local copies, waits for them, and re-layouts: 1.63 us -> none  [the longest x1 0.86 us: on_device(): x_high = velocity[:, :, -1].reshape(3 * depth, span_y)]
    dynamic_slice x1 -> x0, local copies, waits for them, and re-layouts: 1.02 us -> none  [on_device(): give = lax.dynamic_slice_in_dim(acc, (1 - col) * half_x, half_x, 2)]
    ppermute x3, waiting for transfers between devices: 0.01 us -> 0.85 us  [by_core(): return lax.ppermute(x, ('gz', 'col'), pairs)]
  transfers between devices with their start and end apart: 4 -> 4, of which waited for: 1 -> 2; matrix products, arithmetic and copies ran while one was open for 2% -> 1% of each run, Pallas kernels for 33% -> 23%
where the time goes in v2:
time: 56.2 us; the launch traced here: 55.9 us
  starting transfers between devices  22.3 us (40%)
  Pallas kernels  19.5 us (35%)
  blocking collectives  8.64 us (15%)
  waiting for transfers between devices  2.3 us (4%)
  between operations  1.46 us (3%)
  other arithmetic  1.23 us (2%)
    ppermute x3, starting transfers between devices, by_core(): return lax.ppermute(x, ('gz', 'col'), pairs)  20.4 us
    pallas_call x3, Pallas kernels, spread(): pl.pallas_call(kernel, out_shape=pltpu.VMEM((depth, 3 * span_x, span_y),...  13.1 us
    all_gather x1, blocking collectives, on_device(): both = lax.all_gather(sent, 'col', axis=0, tiled=False)  8.64 us
    pallas_call x1, Pallas kernels, spread_last(): pl.pallas_call(kernel, out_shape=(pltpu.VMEM((rows, span_y), jnp.float32)...  5.24 us
    ppermute x1, starting transfers between devices, on_device(): swapped = lax.ppermute(give, 'col', [(0, 1), (1, 0)])  1.92 us
    ppermute x1, waiting for transfers between devices, on_device(): swapped = lax.ppermute(give, 'col', [(0, 1), (1, 0)])  1.45 us
    pallas_call x1, Pallas kernels, pack(): pl.pallas_call(kernel, out_shape=(pltpu.VMEM((total, span_y), jnp.float32...  1.15 us
    add x1, other arithmetic, on_device(): velocity_next = velocity + viscous * (neighbours - 6.0 * velocity) + force  1.13 us
  transfers between devices with their start and end apart: 4, of which 2 were waited for; matrix products, arithmetic and copies ran while one was open for 1% of the time, Pallas kernels for 23%

profile of v2, /device:TPU:1, one launch (start us, length us, event | category | flops | bytes accessed | tf_op | source)
XLA Modules:
  0.0 55.9 jit_solution(18239989220173977271)
XLA Ops:
  1.3 1.2 %pack.1 = (f32[504,128]{1,0:T(8,128)S(1)}, f32[192,128]{1,0:T(8,128)S(1)}) custom-call(s32[1]{0:T(128)} %bitcast.1.col_ref, s32[1]{0:T(128)S(6)} %copy.15.start_ref, f32[4,3,64,128]{3,2,1,0:T(8,128)} %v_ref.1, f32[3,4096]{1,0:T(4,128)} %f_ref.1, f32[3,4096]{1,0:T(4,128)} %o_ref.1, s32[32,128]{1,0:T(8,128)} %bitcast.20, s32[32,128]{1,0:T(8,128)} %bitcast.21, ...), custom_call_target="tpu_custom_call" | custom-call | tf_op jit(solution)/shard_map/pack/pallas_call | solution.py:234
  2.4 8.6 %all-gather = f32[1008,128]{1,0:T(8,128)S(1)} all-gather(f32[504,128]{1,0:T(8,128)S(1)} %get-tuple-element.6.refs_1_), channel_id=2, replica_groups=mesh['gz'=256,'col'=2] {'col'}, dimensions={0}, use_global_device_ids=true | all-gather | bytes 774144 | tf_op jit(solution)/shard_map/all_gather | solution.py:273
  11.1 11.2 %collective-permute-start = (f32[576,128]{1,0:T(8,128)S(1)}, f32[576,128]{1,0:T(8,128)S(1)}, u32[]{:S(2)}, u32[]{:S(2)}) collective-permute-start(f32[576,128]{1,0:T(8,128)S(1)} %bitcast.16), channel_id=1, source_target_pairs={{0,4},{1,509},{2,6},{3,511},{4,8},{5,1},{6,10},{7,3},{8,12},{9,5},... | collective-permute-start | bytes 884744 | tf_op jit(solution)/shard_map/ppermute | solution.py:260
  22.4 3.0 %collective-permute-start.2 = (f32[960,128]{1,0:T(8,128)S(1)}, f32[960,128]{1,0:T(8,128)S(1)}, u32[]{:S(2)}, u32[]{:S(2)}) collective-permute-start(f32[960,128]{1,0:T(8,128)S(1)} %pad_maximum_fusion), channel_id=1, source_target_pairs={{0,2},{1,511},{2,4},{3,1},{4,6},{5,3},{6,8},{7,5},{8,10},{9,7},{10... | collective-permute-start | bytes 1474568 | tf_op jit(solution)/shard_map/ppermute | solution.py:260
  25.5 2.9 %spread.3.refs_2_ = f32[4,384,128]{2,1,0:T(8,128)S(1)} custom-call(f32[1]{0:T(128)} %bitcast.refs_0_.plane_ref, f32[504,128]{1,0:T(8,128)S(1)} %get-tuple-element.6.refs_1_), custom_call_target="tpu_custom_call" | custom-call | flops 1610612736 | bytes 2000000 | tf_op jit(solution)/shard_map/spread/pallas_call | solution.py:167
  28.3 0.8 %collective-permute-done.refs_1_ = f32[576,128]{1,0:T(8,128)S(1)} collective-permute-done((f32[576,128]{1,0:T(8,128)S(1)}, f32[576,128]{1,0:T(8,128)S(1)}, u32[]{:S(2)}, u32[]{:S(2)}) %collective-permute-start) | collective-permute-done | bytes 294944 | tf_op jit(solution)/shard_map/ppermute | solution.py:260
  29.2 6.2 %collective-permute-start.1 = (f32[576,128]{1,0:T(8,128)S(1)}, f32[576,128]{1,0:T(8,128)S(1)}, u32[]{:S(2)}, u32[]{:S(2)}) collective-permute-start(f32[576,128]{1,0:T(8,128)S(1)} %collective-permute-done.refs_1_), channel_id=1, source_target_pairs={{0,2},{1,511},{2,4},{3,1},{4,6},{5,3},{6,8},{7,5},{8,10},{9,7},{10... | collective-permute-start | bytes 884744 | tf_op jit(solution)/shard_map/ppermute | solution.py:260
  35.4 5.1 %spread.4.refs_2_ = f32[4,384,128]{2,1,0:T(8,128)S(1)} custom-call(f32[1]{0:T(128)} %bitcast.refs_0_.plane_ref, f32[576,128]{1,0:T(8,128)S(1)} %collective-permute-done.refs_1_, f32[4,384,128]{2,1,0:T(8,128)S(1)} %spread.3.refs_2_), custom_call_target="tpu_custom_call", output_to_operand_aliasing={{}: (2, {})} | custom-call | flops 3221225472 | bytes 2000000 | tf_op jit(solution)/shard_map/spread/pallas_call | solution.py:167
  40.5 0.0 collective-permute-done.2.refs_1_.near_ref
  40.6 5.1 %spread.5.in_ref = f32[4,384,128]{2,1,0:T(8,128)S(1)} custom-call(f32[1]{0:T(128)} %bitcast.refs_0_.plane_ref, f32[960,128]{1,0:T(8,128)S(1)} %collective-permute-done.2.refs_1_.near_ref, f32[4,384,128]{2,1,0:T(8,128)S(1)} %spread.4.refs_2_), custom_call_target="tpu_custom_call", output_to_operand_aliasing={{}: (2, {})} | custom-call | flops 3221225472 | bytes 2000000 | tf_op jit(solution)/shard_map/spread/pallas_call | solution.py:167
  45.7 0.0 collective-permute-done.1.list_ref
  45.7 0.0 copy-start
  45.7 5.2 %spread_last.1 = (f32[768,128]{1,0:T(8,128)S(1)}, f32[960,128]{1,0:T(8,128)S(1)}) custom-call(f32[1]{0:T(128)} %bitcast.refs_0_.plane_ref, s32[1]{0:T(128)} %bitcast.1.col_ref, f32[576,128]{1,0:T(8,128)S(1)} %collective-permute-done.1.list_ref, f32[4,384,128]{2,1,0:T(8,128)S(1)} %spread.5.in_ref, f32[960,128]{1,0:T(8,128)S(1)} %collective-permute-done.2.refs_1_.near_ref), custom_call_target="tpu_custom_call" | custom-call | flops 3221225472 | bytes 2000000 | tf_op jit(solution)/shard_map/spread_last/pallas_call | solution.py:197
  51.0 1.9 %collective-permute-start.3 = (f32[960,128]{1,0:T(8,128)S(1)}, f32[960,128]{1,0:T(8,128)S(1)}, u32[]{:S(2)}, u32[]{:S(2)}) collective-permute-start(f32[960,128]{1,0:T(8,128)S(1)} %get-tuple-element.9), channel_id=1, source_target_pairs={{0,1},{1,0},{2,3},{3,2},{4,5},{5,4},{6,7},{7,6},{8,9},{9,8},{10,11... | collective-permute-start | bytes 1474568 | tf_op jit(solution)/shard_map/ppermute | solution.py:290
  52.9 0.0 copy-done
  52.9 0.2 fusion.10
  53.1 0.2 fusion.9
  53.3 1.5 %collective-permute-done.3 = f32[960,128]{1,0:T(8,128)S(1)} collective-permute-done((f32[960,128]{1,0:T(8,128)S(1)}, f32[960,128]{1,0:T(8,128)S(1)}, u32[]{:S(2)}, u32[]{:S(2)}) %collective-permute-start.3) | collective-permute-done | bytes 491552 | tf_op jit(solution)/shard_map/ppermute | solution.py:290
  54.8 0.0 copy-start.1
  54.8 1.1 %fusion.6 = f32[4,3,64,128]{3,2,1,0:T(8,128)} fusion(f32[4,3,64,128]{3,2,1,0:T(8,128)S(1)} %bitcast.14, f32[4,3,64,128]{3,2,1,0:T(8,128)S(1)} %copy-done, f32[4,3,1,128]{3,2,1,0:T(1,128)S(1)} %reshape.51, f32[4,3,1,128]{3,2,1,0:T(1,128)S(1)} %reshape.50, f32[1,3,64,128]{3,2,1,0:T(8,128)S(1)} %bitcast.19, f32[1,3,64,128]{3,2,1,0:T(8,128)S(1)} %bitcast.18, ...), kind=kLoop, calls=%fused_computation.8 | loop fusion | flops 1572864 | bytes 2174976 | tf_op jit(solution)/shard_map/add | solution.py:300
  55.9 0.0 copy-done.1
  (9 shorter events, 0.2 us)
Async XLA Ops:
  11.1 18.1 %collective-permute-start = (f32[576,128]{1,0:T(8,128)S(1)}, f32[576,128]{1,0:T(8,128)S(1)}, u32[]{:S(2)}, u32[]{:S(2)}) collective-permute-start(f32[576,128]{1,0:T(8,128)S(1)} %bitcast.16), channel_id=1, source_target_pairs={{0,4},{1,509},{2,6},{3,511},{4,8},{5,1},{6,10},{7,3},{8,12},{9,5},... | collective-permute-start | bytes 884744 | tf_op jit(solution)/shard_map/ppermute | solution.py:260
  22.4 18.1 %collective-permute-start.2 = (f32[960,128]{1,0:T(8,128)S(1)}, f32[960,128]{1,0:T(8,128)S(1)}, u32[]{:S(2)}, u32[]{:S(2)}) collective-permute-start(f32[960,128]{1,0:T(8,128)S(1)} %pad_maximum_fusion), channel_id=1, source_target_pairs={{0,2},{1,511},{2,4},{3,1},{4,6},{5,3},{6,8},{7,5},{8,10},{9,7},{10... | collective-permute-start | bytes 1474568 | tf_op jit(solution)/shard_map/ppermute | solution.py:260
  29.2 16.5 %collective-permute-start.1 = (f32[576,128]{1,0:T(8,128)S(1)}, f32[576,128]{1,0:T(8,128)S(1)}, u32[]{:S(2)}, u32[]{:S(2)}) collective-permute-start(f32[576,128]{1,0:T(8,128)S(1)} %collective-permute-done.refs_1_), channel_id=1, source_target_pairs={{0,2},{1,511},{2,4},{3,1},{4,6},{5,3},{6,8},{7,5},{8,10},{9,7},{10... | collective-permute-start | bytes 884744 | tf_op jit(solution)/shard_map/ppermute | solution.py:260
  45.7 7.2 %copy-start = (f32[4,3,64,128]{3,2,1,0:T(8,128)S(1)}, f32[4,3,64,128]{3,2,1,0:T(8,128)}, u32[]{:S(2)}) copy-start(f32[4,3,64,128]{3,2,1,0:T(8,128)} %v_ref.1) | copy-start | bytes 1179652
  51.0 3.8 %collective-permute-start.3 = (f32[960,128]{1,0:T(8,128)S(1)}, f32[960,128]{1,0:T(8,128)S(1)}, u32[]{:S(2)}, u32[]{:S(2)}) collective-permute-start(f32[960,128]{1,0:T(8,128)S(1)} %get-tuple-element.9), channel_id=1, source_target_pairs={{0,1},{1,0},{2,3},{3,2},{4,5},{5,4},{6,7},{7,6},{8,9},{9,8},{10,11... | collective-permute-start | bytes 1474568 | tf_op jit(solution)/shard_map/ppermute | solution.py:290
  54.8 1.1 %copy-start.1 = (f32[768,128]{1,0:T(8,128)}, f32[768,128]{1,0:T(8,128)S(1)}, u32[]{:S(2)}) copy-start(f32[768,128]{1,0:T(8,128)S(1)} %slice_add_fusion) | copy-start | bytes 1179652

commit v3 on v2

--- a/solution.py
+++ b/solution.py
@@ -10,6 +10,7 @@
 ATTRS = 9
 LIST = ROWS * ATTRS
 KROWS = 8
+KERNEL_VMEM = 16 << 20
 SLOTS = 24
 TILE = 16
 
@@ -105,7 +106,18 @@
                 b_ref[pl.ds(z * span_y + t * TILE, TILE), lanes] = jnp.where(here, b_rows[z], nothing)
 
 
-def spread_lists(list_ref, lists, first_plane, acc_ref, dims, rows_ref, bufs):
+def spread_lists(list_ref, lists, first_plane, acc_ref, dims, rows_ref):
+    depth, span_x, span_y, _ = dims
+    a = pltpu.VMEM((3 * span_x, KROWS * 128), jnp.bfloat16)
+    b = pltpu.VMEM((depth * span_y, KROWS * 128), jnp.bfloat16)
+
+    def run(a0, b0, a1, b1):
+        spread_turns(list_ref, lists, first_plane, acc_ref, dims, rows_ref, ((a0, b0), (a1, b1)))
+
+    pl.run_scoped(run, a, b, a, b)
+
+
+def spread_turns(list_ref, lists, first_plane, acc_ref, dims, rows_ref, bufs):
     depth, span_x, span_y, _ = dims
     turns = lists * (ROWS // KROWS)
     for n in range(lists):
@@ -134,11 +146,8 @@
     lax.fori_loop(0, turns // 2, two_turns, 0)
 
 
-def scratch(lists, dims):
-    depth, span_x, span_y, _ = dims
-    a = pltpu.VMEM((3 * span_x, KROWS * 128), jnp.bfloat16)
-    b = pltpu.VMEM((depth * span_y, KROWS * 128), jnp.bfloat16)
-    return [pltpu.VMEM((lists * SLOTS * ROWS, 128), jnp.float32), a, b, a, b]
+def scratch(lists):
+    return [pltpu.VMEM((lists * SLOTS * ROWS, 128), jnp.float32)]
 
 
 def cost(lists, dims):
@@ -150,28 +159,35 @@
     )
 
 
-def spread(markers, lists, acc, plane, dims):
+def spread(markers, lists, acc, plane, dims, after=None):
     depth, span_x, span_y, _ = dims
 
     def kernel(*refs):
         if acc is None:
-            plane_ref, list_ref, out_ref, rows_ref, a0, b0, a1, b1 = refs
+            plane_ref, list_ref, out_ref, token_ref, rows_ref = refs
             out_ref[...] = jnp.zeros_like(out_ref)
         else:
-            plane_ref, list_ref, _, out_ref, rows_ref, a0, b0, a1, b1 = refs
-        spread_lists(list_ref, lists, plane_ref[0], out_ref, dims, rows_ref, ((a0, b0), (a1, b1)))
+            plane_ref, list_ref, out_ref, token_ref, rows_ref = refs[:2] + refs[-3:]
+        token_ref[...] = jnp.zeros_like(token_ref)
+        spread_lists(list_ref, lists, plane_ref[0], out_ref, dims, rows_ref)
 
     operands = (plane, in_vmem(markers))
     if acc is not None:
         operands += (in_vmem(acc),)
+    if after is not None:
+        operands += (in_vmem(after),)
     return pl.pallas_call(
         kernel,
-        out_shape=pltpu.VMEM((depth, 3 * span_x, span_y), jnp.float32),
+        out_shape=(
+            pltpu.VMEM((depth, 3 * span_x, span_y), jnp.float32),
+            pltpu.VMEM((8, 128), jnp.float32),
+        ),
         in_specs=[smem()] + [vmem()] * (len(operands) - 1),
-        out_specs=vmem(),
+        out_specs=(vmem(), vmem()),
         input_output_aliases={} if acc is None else {2: 0},
-        scratch_shapes=scratch(lists, dims),
+        scratch_shapes=scratch(lists),
         cost_estimate=cost(lists, dims),
+        compiler_params=pltpu.CompilerParams(vmem_limit_bytes=KERNEL_VMEM),
         name="spread",
     )(*operands)
 
@@ -182,10 +198,10 @@
     rows = depth * 3 * half
     plane_at = 2 * LIST + 3 * half
 
-    def kernel(plane_ref, col_ref, list_ref, in_ref, near_ref, keep_ref, give_ref, acc_ref, rows_ref, a0, b0, a1, b1):
+    def kernel(plane_ref, col_ref, list_ref, in_ref, near_ref, keep_ref, give_ref, acc_ref, rows_ref):
         acc_ref[...] = in_ref[...]
         give_ref[pl.ds(rows, 3 * half), :] = near_ref[pl.ds(plane_at, 3 * half), :]
-        spread_lists(list_ref, lists, plane_ref[0], acc_ref, dims, rows_ref, ((a0, b0), (a1, b1)))
+        spread_lists(list_ref, lists, plane_ref[0], acc_ref, dims, rows_ref)
         mine = pl.multiple_of(col_ref[0] * half, half)
         other = pl.multiple_of((1 - col_ref[0]) * half, half)
         for z in range(depth):
@@ -202,8 +218,9 @@
         ),
         in_specs=[smem(), smem(), vmem(), vmem(), vmem()],
         out_specs=(vmem(), vmem()),
-        scratch_shapes=[pltpu.VMEM((depth, 3 * span_x, span_y), jnp.float32)] + scratch(lists, dims),
+        scratch_shapes=[pltpu.VMEM((depth, 3 * span_x, span_y), jnp.float32)] + scratch(lists),
         cost_estimate=cost(lists, dims),
+        compiler_params=pltpu.CompilerParams(vmem_limit_bytes=KERNEL_VMEM),
         name="spread_last",
     )(plane, col, in_vmem(markers), in_vmem(acc), in_vmem(nearest))
 
@@ -277,14 +294,14 @@
     partner_low = partner[plane_rows : plane_rows + 3 * depth].reshape(depth, 3, 1, span_y)
     partner_high = partner[plane_rows + 3 * depth :].reshape(depth, 3, 1, span_y)
 
+    slab = (gz_index * depth).astype(jnp.float32).reshape(1)
+    nearest = by_core(jnp.concatenate([chip, plane_out]), gz_count, 1)
     second = by_core(chip, gz_count, 2)
-    nearest = by_core(jnp.concatenate([chip, plane_out]), gz_count, 1)
+    acc, _ = spread(sent, 1, None, slab, dims)
+    acc, token = spread(nearest, 2, acc, slab, dims)
+    second, token = lax.optimization_barrier((second, token))
     third = by_core(second, gz_count, 1)
-
-    slab = (gz_index * depth).astype(jnp.float32).reshape(1)
-    acc = spread(sent, 1, None, slab, dims)
-    acc = spread(second, 2, acc, slab, dims)
-    acc = spread(nearest, 2, acc, slab, dims)
+    acc, _ = spread(second, 2, acc, slab, dims, token)
     keep, give = spread_last(third, 2, acc, nearest, slab, core, dims)
     my_plane = nearest[2 * LIST : 2 * LIST + plane_rows]
     swapped = lax.ppermute(give, "col", [(0, 1), (1, 0)])

time: 56.2 us -> 58.1 us (1.034)
  starting transfers between devices: 22.3 us -> 26.4 us
  Pallas kernels: 19.5 us -> 17.3 us
    ppermute x1, starting transfers between devices: 1.92 us -> 4.29 us  [on_device(): swapped = lax.ppermute(give, 'col', [(0, 1), (1, 0)])]
    ppermute x3, starting transfers between devices: 20.4 us -> 22.1 us  [by_core(): return lax.ppermute(x, ('gz', 'col'), pairs)]
    pallas_call x3, Pallas kernels: 13.1 us -> 11.5 us  [spread(): pl.pallas_call(kernel, out_shape=(pltpu.VMEM((depth, 3 * span_x, span_y),...]
    pallas_call x1, Pallas kernels: 5.24 us -> 4.64 us  [spread_last(): pl.pallas_call(kernel, out_shape=(pltpu.VMEM((rows, span_y), jnp.float32)...]
  transfers between devices with their start and end apart: 4 -> 4, of which waited for: 2 -> 2; matrix products, arithmetic and copies ran while one was open for 1% -> 1% of each run, Pallas kernels for 23% -> 20%
where the time goes in v3:
time: 58.1 us; the launch traced here: 57.9 us
  starting transfers between devices  26.4 us (45%)
  Pallas kernels  17.3 us (30%)
  blocking collectives  8.64 us (15%)
  waiting for transfers between devices  2.32 us (4%)
  between operations  1.45 us (2%)
  other arithmetic  1.24 us (2%)
    ppermute x3, starting transfers between devices, by_core(): return lax.ppermute(x, ('gz', 'col'), pairs)  22.1 us
    pallas_call x3, Pallas kernels, spread(): pl.pallas_call(kernel, out_shape=(pltpu.VMEM((depth, 3 * span_x, span_y),...  11.5 us
    all_gather x1, blocking collectives, on_device(): both = lax.all_gather(sent, 'col', axis=0, tiled=False)  8.64 us
    pallas_call x1, Pallas kernels, spread_last(): pl.pallas_call(kernel, out_shape=(pltpu.VMEM((rows, span_y), jnp.float32)...  4.64 us
    ppermute x1, starting transfers between devices, on_device(): swapped = lax.ppermute(give, 'col', [(0, 1), (1, 0)])  4.29 us
    ppermute x3, waiting for transfers between devices, by_core(): return lax.ppermute(x, ('gz', 'col'), pairs)  1.23 us
  transfers between devices with their start and end apart: 4, of which 2 were waited for; matrix products, arithmetic and copies ran while one was open for 1% of the time, Pallas kernels for 20%

profile of v3, /device:TPU:1, one launch (start us, length us, event | category | flops | bytes accessed | tf_op | source)
XLA Modules:
  0.0 57.9 jit_solution(7131286280994567851)
XLA Ops:
  1.3 1.2 %pack.1 = (f32[504,128]{1,0:T(8,128)S(1)}, f32[192,128]{1,0:T(8,128)S(1)}) custom-call(s32[1]{0:T(128)} %bitcast.1.col_ref, s32[1]{0:T(128)S(6)} %copy.15.start_ref, f32[4,3,64,128]{3,2,1,0:T(8,128)} %v_ref.1, f32[3,4096]{1,0:T(4,128)} %f_ref.1, f32[3,4096]{1,0:T(4,128)} %o_ref.1, s32[32,128]{1,0:T(8,128)} %bitcast.20, s32[32,128]{1,0:T(8,128)} %bitcast.21, ...), custom_call_target="tpu_custom_call" | custom-call | tf_op jit(solution)/shard_map/pack/pallas_call | solution.py:251
  2.4 8.6 %all-gather = f32[1008,128]{1,0:T(8,128)S(1)} all-gather(f32[504,128]{1,0:T(8,128)S(1)} %get-tuple-element.12.refs_1_), channel_id=2, replica_groups=mesh['gz'=256,'col'=2] {'col'}, dimensions={0}, use_global_device_ids=true | all-gather | bytes 774144 | tf_op jit(solution)/shard_map/all_gather | solution.py:290
  11.2 10.4 %collective-permute-start.1 = (f32[960,128]{1,0:T(8,128)S(1)}, f32[960,128]{1,0:T(8,128)S(1)}, u32[]{:S(2)}, u32[]{:S(2)}) collective-permute-start(f32[960,128]{1,0:T(8,128)S(1)} %pad_maximum_fusion), channel_id=1, source_target_pairs={{0,2},{1,511},{2,4},{3,1},{4,6},{5,3},{6,8},{7,5},{8,10},{9,7},{10... | collective-permute-start | bytes 1474568 | tf_op jit(solution)/shard_map/ppermute | solution.py:277
  21.6 3.8 %collective-permute-start = (f32[576,128]{1,0:T(8,128)S(1)}, f32[576,128]{1,0:T(8,128)S(1)}, u32[]{:S(2)}, u32[]{:S(2)}) collective-permute-start(f32[576,128]{1,0:T(8,128)S(1)} %bitcast.17), channel_id=1, source_target_pairs={{0,4},{1,509},{2,6},{3,511},{4,8},{5,1},{6,10},{7,3},{8,12},{9,5},... | collective-permute-start | bytes 884744 | tf_op jit(solution)/shard_map/ppermute | solution.py:277
  25.5 2.5 %spread.3 = (f32[4,384,128]{2,1,0:T(8,128)S(1)}, f32[8,128]{1,0:T(8,128)}) custom-call(f32[1]{0:T(128)} %bitcast.refs_0_.plane_ref, f32[504,128]{1,0:T(8,128)S(1)} %get-tuple-element.12.refs_1_), custom_call_target="tpu_custom_call" | custom-call | flops 1610612736 | bytes 2000000 | tf_op jit(solution)/shard_map/spread/pallas_call | solution.py:179
  27.9 0.0 collective-permute-done.1.refs_1_.near_ref
  27.9 4.5 %spread.4 = (f32[4,384,128]{2,1,0:T(8,128)S(1)}, f32[8,128]{1,0:T(8,128)S(1)}) custom-call(f32[1]{0:T(128)} %bitcast.refs_0_.plane_ref, f32[960,128]{1,0:T(8,128)S(1)} %collective-permute-done.1.refs_1_.near_ref, f32[4,384,128]{2,1,0:T(8,128)S(1)} %get-tuple-element.14.refs_2_), custom_call_target="tpu_custom_call", output_to_operand_aliasing={{0}: (2, {})} | custom-call | flops 3221225472 | bytes 2000000 | tf_op jit(solution)/shard_map/spread/pallas_call | solution.py:179
  32.5 1.2 %collective-permute-done.refs_1_ = f32[576,128]{1,0:T(8,128)S(1)} collective-permute-done((f32[576,128]{1,0:T(8,128)S(1)}, f32[576,128]{1,0:T(8,128)S(1)}, u32[]{:S(2)}, u32[]{:S(2)}) %collective-permute-start) | collective-permute-done | bytes 294944 | tf_op jit(solution)/shard_map/ppermute | solution.py:277
  33.7 7.9 %collective-permute-start.2 = (f32[576,128]{1,0:T(8,128)S(1)}, f32[576,128]{1,0:T(8,128)S(1)}, u32[]{:S(2)}, u32[]{:S(2)}) collective-permute-start(f32[576,128]{1,0:T(8,128)S(1)} %collective-permute-done.refs_1_), channel_id=1, source_target_pairs={{0,2},{1,511},{2,4},{3,1},{4,6},{5,3},{6,8},{7,5},{8,10},{9,7},{10... | collective-permute-start | bytes 884744 | tf_op jit(solution)/shard_map/ppermute | solution.py:277
  41.7 4.5 %spread.5 = (f32[4,384,128]{2,1,0:T(8,128)S(1)}, f32[8,128]{1,0:T(8,128)}) custom-call(f32[1]{0:T(128)} %bitcast.refs_0_.plane_ref, f32[576,128]{1,0:T(8,128)S(1)} %collective-permute-done.refs_1_, f32[4,384,128]{2,1,0:T(8,128)S(1)} %get-tuple-element.17.refs_2_, f32[8,128]{1,0:T(8,128)S(1)} %get-tuple-element.18.refs_3_), custom_call_target="tpu_custom_call", output_to_operand_aliasing={{0}: (2, {})} | custom-call | flops 3221225472 | bytes 2000000 | tf_op jit(solution)/shard_map/spread/pallas_call | solution.py:179
  46.2 0.0 collective-permute-done.2.list_ref
  46.2 0.0 copy-start
  46.2 4.6 %spread_last.1 = (f32[768,128]{1,0:T(8,128)S(1)}, f32[960,128]{1,0:T(8,128)S(1)}) custom-call(f32[1]{0:T(128)} %bitcast.refs_0_.plane_ref, s32[1]{0:T(128)} %bitcast.1.col_ref, f32[576,128]{1,0:T(8,128)S(1)} %collective-permute-done.2.list_ref, f32[4,384,128]{2,1,0:T(8,128)S(1)} %get-tuple-element.19.in_ref, ...), custom_call_target="tpu_custom_call" | custom-call | flops 3221225472 | bytes 2000000 | tf_op jit(solution)/shard_map/spread_last/pallas_call | solution.py:213
  50.9 4.3 %collective-permute-start.3 = (f32[960,128]{1,0:T(8,128)S(1)}, f32[960,128]{1,0:T(8,128)S(1)}, u32[]{:S(2)}, u32[]{:S(2)}) collective-permute-start(f32[960,128]{1,0:T(8,128)S(1)} %get-tuple-element.21), channel_id=1, source_target_pairs={{0,1},{1,0},{2,3},{3,2},{4,5},{5,4},{6,7},{7,6},{8,9},{9,8},{10,11... | collective-permute-start | bytes 1474568 | tf_op jit(solution)/shard_map/ppermute | solution.py:307
  55.2 0.0 copy-done
  55.2 0.2 fusion.10
  55.4 0.2 fusion.9
  55.5 1.1 %collective-permute-done.3 = f32[960,128]{1,0:T(8,128)S(1)} collective-permute-done((f32[960,128]{1,0:T(8,128)S(1)}, f32[960,128]{1,0:T(8,128)S(1)}, u32[]{:S(2)}, u32[]{:S(2)}) %collective-permute-start.3) | collective-permute-done | bytes 491552 | tf_op jit(solution)/shard_map/ppermute | solution.py:307
  56.7 0.1 slice_add_fusion
  56.7 0.0 copy-start.1
  56.7 1.1 %fusion.6 = f32[4,3,64,128]{3,2,1,0:T(8,128)} fusion(f32[4,3,64,128]{3,2,1,0:T(8,128)S(1)} %bitcast.14, f32[4,3,64,128]{3,2,1,0:T(8,128)S(1)} %copy-done, f32[4,3,1,128]{3,2,1,0:T(1,128)S(1)} %reshape.51, f32[4,3,1,128]{3,2,1,0:T(1,128)S(1)} %reshape.50, f32[1,3,64,128]{3,2,1,0:T(8,128)S(1)} %bitcast.19, f32[1,3,64,128]{3,2,1,0:T(8,128)S(1)} %bitcast.18, ...), kind=kLoop, calls=%fused_computation.8 | loop fusion | flops 1572864 | bytes 2174976 | tf_op jit(solution)/shard_map/add | solution.py:317
  57.9 0.0 copy-done.1
  (8 shorter events, 0.1 us)
Async XLA Ops:
  11.2 16.7 %collective-permute-start.1 = (f32[960,128]{1,0:T(8,128)S(1)}, f32[960,128]{1,0:T(8,128)S(1)}, u32[]{:S(2)}, u32[]{:S(2)}) collective-permute-start(f32[960,128]{1,0:T(8,128)S(1)} %pad_maximum_fusion), channel_id=1, source_target_pairs={{0,2},{1,511},{2,4},{3,1},{4,6},{5,3},{6,8},{7,5},{8,10},{9,7},{10... | collective-permute-start | bytes 1474568 | tf_op jit(solution)/shard_map/ppermute | solution.py:277
  21.6 12.1 %collective-permute-start = (f32[576,128]{1,0:T(8,128)S(1)}, f32[576,128]{1,0:T(8,128)S(1)}, u32[]{:S(2)}, u32[]{:S(2)}) collective-permute-start(f32[576,128]{1,0:T(8,128)S(1)} %bitcast.17), channel_id=1, source_target_pairs={{0,4},{1,509},{2,6},{3,511},{4,8},{5,1},{6,10},{7,3},{8,12},{9,5},... | collective-permute-start | bytes 884744 | tf_op jit(solution)/shard_map/ppermute | solution.py:277
  33.7 12.5 %collective-permute-start.2 = (f32[576,128]{1,0:T(8,128)S(1)}, f32[576,128]{1,0:T(8,128)S(1)}, u32[]{:S(2)}, u32[]{:S(2)}) collective-permute-start(f32[576,128]{1,0:T(8,128)S(1)} %collective-permute-done.refs_1_), channel_id=1, source_target_pairs={{0,2},{1,511},{2,4},{3,1},{4,6},{5,3},{6,8},{7,5},{8,10},{9,7},{10... | collective-permute-start | bytes 884744 | tf_op jit(solution)/shard_map/ppermute | solution.py:277
  46.2 9.0 %copy-start = (f32[4,3,64,128]{3,2,1,0:T(8,128)S(1)}, f32[4,3,64,128]{3,2,1,0:T(8,128)}, u32[]{:S(2)}) copy-start(f32[4,3,64,128]{3,2,1,0:T(8,128)} %v_ref.1) | copy-start | bytes 1179652
  50.9 5.8 %collective-permute-start.3 = (f32[960,128]{1,0:T(8,128)S(1)}, f32[960,128]{1,0:T(8,128)S(1)}, u32[]{:S(2)}, u32[]{:S(2)}) collective-permute-start(f32[960,128]{1,0:T(8,128)S(1)} %get-tuple-element.21), channel_id=1, source_target_pairs={{0,1},{1,0},{2,3},{3,2},{4,5},{5,4},{6,7},{7,6},{8,9},{9,8},{10,11... | collective-permute-start | bytes 1474568 | tf_op jit(solution)/shard_map/ppermute | solution.py:307
  56.7 1.1 %copy-start.1 = (f32[768,128]{1,0:T(8,128)}, f32[768,128]{1,0:T(8,128)S(1)}, u32[]{:S(2)}) copy-start(f32[768,128]{1,0:T(8,128)S(1)} %slice_add_fusion) | copy-start | bytes 1179652
